TPU v7x, 256 devices: a whole 4x4x8 slice. The times are simulated.
256 devices in a mesh: row: 32 (over y, x, core), col: 8 (over z).
Axes of the slice: x: 4, y: 4, z: 8, core: 2. Of those that a mesh axis runs over, the one named last changes fastest.
Arguments:
- right_side: float32 [2, 8192, 2048], P(None, 'row', 'col'), may hold values from -6 to 6
- probe: float32 [2, 256, 256], replicated, may hold values from -6 to 6
- detector_weights: float32 [256, 256], replicated, may hold values from 0.1 to 10
- offsets: int32 [32, 8, 4, 2], P('row', 'col'), may hold values from -128 to 127, as said below
- counts: int32 [32, 8], P('row', 'col'), may hold values from 2 to 4, as said below
Outputs:
- solution_field: float32 [2, 8192, 2048], P(None, 'row', 'col')
- residual: float32 [2, 8192, 2048], P(None, 'row', 'col')
Inputs may be any that keep to these rules, and one draw needn't show every extreme that they name: `counts`: every region holds at least two positions; in every draw some region holds exactly 4. In every region slot 0 has both offsets negative and slot 1 both offsets non-negative.
All inputs are finite; a program needn't handle non-finite values.
Results may differ from a plain program's by a relative error of at most 0.0003.
Values sent between devices are 32-bit elements; how exact they have to be, the bound alone decides.
A program may use at most 64 MiB of HBM per device.

v0:
```python
import functools
import math

import jax
import jax.numpy as jnp
import numpy as np
from jax import lax
from jax.experimental import pallas as pl
from jax.experimental.pallas import tpu as pltpu
from jax.sharding import PartitionSpec as P

ITERS = 3
ridge_weight = 0.5
MESH = pl.DeviceIdType.MESH
f32 = jnp.float32
bf16 = jnp.bfloat16


def tables(side):
    half = side // 2
    n = np.arange(half)
    found = []
    for odd in (0, 1):
        phase = ((2 * np.arange(half) + odd)[:, None] * n[None, :]) % side
        angle = phase * (-2.0 * math.pi / side)
        re, im = np.cos(angle) / math.sqrt(side), np.sin(angle) / math.sqrt(side)
        found.append(np.block([[re, -im], [im, re]]).astype(np.float32))
    full = found + [mat.T.copy() for mat in found]
    out = []
    for mat in full:
        hi = mat.astype(jnp.bfloat16)
        out += [hi, (mat - hi.astype(np.float32)).astype(jnp.bfloat16)]
    return np.stack(out)


def split(value):
    hi = value.astype(bf16)
    return hi, (value - hi.astype(f32)).astype(bf16)


def dot(left, right):
    return jnp.dot(left, right, preferred_element_type=f32)


def dot3(left, right):
    return dot(left[0], right[0]) + (dot(left[0], right[1]) + dot(left[1], right[0]))


def kernel(n_row, n_col, cap, right_ref, probe_ref, weights_ref, mats_ref, offs_ref, count_ref,
           x_out, r_out,
           field, halo_r, halo_c, halo_x, acc_o, acc_r, acc_c, acc_x, back_r, back_c, back_x,
           illum, spec_hi, spec_lo, wave_hi, wave_lo, wgt, x_ref, d_ref, along_ref, quad_ref,
           scal_ref, msg1, msg2, gs, gr, bs, br, as_, ar):
    side = field.shape[1]
    half = side // 2
    row, col = lax.axis_index("row"), lax.axis_index("col")
    odd = lax.rem(row, 2)
    near = row + 1 - 2 * odd
    far = row - 1 + 2 * odd
    has_far = jnp.logical_and(far >= 0, far < n_row)
    has_left, has_right = col > 0, col < n_col - 1
    h_far = pl.multiple_of(odd * half, half)
    h_near = pl.multiple_of(half - odd * half, half)

    for ref in (halo_r, halo_c, halo_x, back_r, back_c, back_x, x_ref, d_ref, along_ref):
        ref[...] = jnp.zeros_like(ref)
    field[...] = right_ref[...]

    barrier = pltpu.get_barrier_semaphore()

    def greet_row(step, carry):
        pl.semaphore_signal(barrier, inc=1, device_id={"row": lax.rem(row + step, n_row)}, device_id_type=MESH)
        return carry

    def greet_col(step, carry):
        pl.semaphore_signal(barrier, inc=1, device_id={"col": lax.rem(col + step, n_col)}, device_id_type=MESH)
        return carry

    lax.fori_loop(1, n_row, greet_row, 0)
    lax.fori_loop(1, n_col, greet_col, 0)
    pl.semaphore_wait(barrier, n_row + n_col - 2)

    def remote(src, dst, sems, rsems, i, target):
        return pltpu.make_async_remote_copy(
            src_ref=src, dst_ref=dst, send_sem=sems.at[i], recv_sem=rsems.at[i],
            device_id=target, device_id_type=MESH)

    def rows_of(ref, start):
        return ref.at[:, pl.ds(start, half), :]

    def block_of(ref, start, col_start):
        return ref.at[:, pl.ds(start, half), pl.ds(col_start, half)]

    def gather_copies():
        left, right = {"col": col - 1}, {"col": col + 1}
        to_left = [remote(block_of(field, h, 0), block_of(halo_c, h, 0), gs, gr, i, left)
                   for i, h in enumerate((h_far, h_near))]
        to_right = [remote(block_of(field, h, half), block_of(halo_c, h, half), gs, gr, 2 + i, right)
                    for i, h in enumerate((h_far, h_near))]
        own_far = remote(rows_of(field, h_far), rows_of(halo_r, h_far), gs, gr, 4, {"row": far})
        own_near = remote(rows_of(field, h_near), rows_of(halo_r, h_near), gs, gr, 5, {"row": near})
        cor_far = remote(rows_of(halo_c, h_far), rows_of(halo_x, h_far), gs, gr, 6, {"row": far})
        cor_near = remote(rows_of(halo_c, h_near), rows_of(halo_x, h_near), gs, gr, 7, {"row": near})
        return to_left, to_right, own_far, own_near, cor_far, cor_near

    def gather(between):
        to_left, to_right, own_far, own_near, cor_far, cor_near = gather_copies()
        for i in (0, 1):
            pl.when(has_left)(to_left[i].start)
            pl.when(has_right)(to_right[i].start)
            if i == 0:
                pl.when(has_far)(own_far.start)
                own_near.start()
        between()
        pl.when(has_right)(to_left[0].wait_recv)
        pl.when(has_left)(to_right[0].wait_recv)
        pl.when(has_far)(cor_far.start)
        pl.when(has_right)(to_left[1].wait_recv)
        pl.when(has_left)(to_right[1].wait_recv)
        cor_near.start()
        pl.when(has_far)(own_far.wait_recv)
        own_near.wait_recv()
        cor_near.wait_recv()
        pl.when(has_far)(cor_far.wait_recv)

    def gather_done():
        to_left, to_right, own_far, own_near, cor_far, cor_near = gather_copies()
        for i in (0, 1):
            pl.when(has_left)(to_left[i].wait_send)
            pl.when(has_right)(to_right[i].wait_send)
        pl.when(has_far)(own_far.wait_send)
        own_near.wait_send()
        pl.when(has_far)(cor_far.wait_send)
        cor_near.wait_send()

    def prepare():
        ramp_i = lax.broadcasted_iota(jnp.int32, (side, side), 0)
        ramp_j = lax.broadcasted_iota(jnp.int32, (side, side), 1)
        take = jnp.where(ramp_i < half, 2 * ramp_i, 2 * ramp_i + 1 - side)
        left = jnp.where(take == ramp_j, 1.0, 0.0).astype(f32)
        take_t = jnp.where(ramp_j < half, 2 * ramp_j, 2 * ramp_j + 1 - side)
        right = jnp.where(take_t == ramp_i, 1.0, 0.0).astype(f32)
        moved = jnp.dot(left, weights_ref[...], precision=lax.Precision.HIGHEST, preferred_element_type=f32)
        wgt[...] = jnp.dot(moved, right, precision=lax.Precision.HIGHEST, preferred_element_type=f32)

        def place(s, carry):
            down, across = offs_ref[s, 0], offs_ref[s, 1]
            down = jnp.where(down < 0, down + side, down)
            across = jnp.where(across < 0, across + side, across)
            flag = jnp.where(s < count_ref[0, 0], 1.0, 0.0).astype(f32)
            for part in (0, 1):
                rolled = pltpu.roll(probe_ref[part] * flag, down, 0)
                illum[s, part] = pltpu.roll(rolled, across, 1)
            return carry

        lax.fori_loop(0, cap, place, 0)
        scal_ref[0] = jnp.ones_like(scal_ref[0])
        scal_ref[1] = jnp.ones_like(scal_ref[1])
        first = field[...]
        scal_ref[2, 0:1, :] = lanes(jnp.sum(first * first, axis=(0, 1))[None])

    def lanes(value):
        return value[:, :half] + value[:, half:]

    def masks(s, h):
        down, across = offs_ref[s, 0], offs_ref[s, 1]
        t = lax.broadcasted_iota(jnp.int32, (half, half), 0) + h * half
        u = lax.broadcasted_iota(jnp.int32, (half, half), 1)
        row_in = jnp.logical_and(t >= down, t < down + side)
        col_in = (u >= across, u + half < across + side)
        return row_in, col_in

    def forward(s, carry):
        found = []
        for h in (0, 1):
            rows = slice(h * half, (h + 1) * half)
            row_in, col_in = masks(s, h)
            view = []
            for part in (0, 1):
                pieces = []
                for j in (0, 1):
                    cols = slice(j * half, (j + 1) * half)
                    inner = jnp.where(row_in, field[part, rows, cols], halo_r[part, rows, cols])
                    outer = jnp.where(row_in, halo_c[part, rows, cols], halo_x[part, rows, cols])
                    pieces.append(jnp.where(col_in[j], inner, outer))
                view.append(pieces)
            wave = []
            for j in (0, 1):
                cols = slice(j * half, (j + 1) * half)
                pr, pi = illum[s, 0, rows, cols], illum[s, 1, rows, cols]
                vr, vi = view[0][j], view[1][j]
                wave.append((pr * vr - pi * vi, pr * vi + pi * vr))
            plus = jnp.concatenate([wave[0][0] + wave[1][0], wave[0][1] + wave[1][1]], axis=1)
            minus = jnp.concatenate([wave[0][0] - wave[1][0], wave[0][1] - wave[1][1]], axis=1)
            found.append((
                dot3(split(plus), (mats_ref[4], mats_ref[5])),
                dot3(split(minus), (mats_ref[6], mats_ref[7])),
            ))
        quad = jnp.zeros((1, side), f32)
        for which, sign in ((0, 1.0), (1, -1.0)):
            both = [found[0][j] + sign * found[1][j] for j in (0, 1)]
            stacked = jnp.concatenate([
                jnp.concatenate([both[0][:, :half], both[1][:, :half]], axis=1),
                jnp.concatenate([both[0][:, half:], both[1][:, half:]], axis=1)], axis=0)
            freq = dot3((mats_ref[2 * which], mats_ref[2 * which + 1]), split(stacked))
            scale = wgt[which * half:(which + 1) * half, :]
            scaled = freq * jnp.concatenate([scale, scale], axis=0)
            quad = quad + jnp.sum(freq * scaled, axis=0, keepdims=True)
            hi, lo = split(scaled)
            spec_hi[s, which] = hi
            spec_lo[s, which] = lo
        quad_ref[...] += lanes(quad)
        return carry

    def inverse(s, carry):
        even = dot3((mats_ref[4], mats_ref[5]), (spec_hi[s, 0], spec_lo[s, 0]))
        odd_ = dot3((mats_ref[6], mats_ref[7]), (spec_hi[s, 1], spec_lo[s, 1]))
        for h in (0, 1):
            rows = slice(h * half, (h + 1) * half)
            both = even + odd_ if h == 0 else even - odd_
            out = []
            for j in (0, 1):
                cols = slice(j * half, (j + 1) * half)
                lhs = jnp.concatenate([both[:half, cols], both[half:, cols]], axis=1)
                out.append(dot3(split(lhs), (mats_ref[2 * j], mats_ref[2 * j + 1])))
            row_in, col_in = masks(s, h)
            for j in (0, 1):
                cols = slice(j * half, (j + 1) * half)
                mixed = out[0] + out[1] if j == 0 else out[0] - out[1]
                hr, hi = mixed[:, :half], mixed[:, half:]
                pr, pi = illum[s, 0, rows, cols], illum[s, 1, rows, cols]
                for part, term in ((0, pr * hr + pi * hi), (1, pr * hi - pi * hr)):
                    inner = jnp.where(row_in, term, 0.0)
                    outer = term - inner
                    inner_own = jnp.where(col_in[j], inner, 0.0)
                    outer_own = jnp.where(col_in[j], outer, 0.0)
                    acc_o[part, rows, cols] += inner_own
                    acc_c[part, rows, cols] += inner - inner_own
                    acc_r[part, rows, cols] += outer_own
                    acc_x[part, rows, cols] += outer - outer_own
        return carry

    def share(msg, mine, k, count, axis, at, i):
        def send(step, carry):
            remote_to = {axis: lax.rem(mine + step, count)}
            pltpu.make_async_remote_copy(
                src_ref=msg.at[k, mine], dst_ref=msg.at[k, mine], send_sem=as_.at[i, k], recv_sem=ar.at[i, k],
                device_id=remote_to, device_id_type=MESH).start()
            return carry
        msg[k, at] = scal_ref[2]
        lax.fori_loop(1, count, send, 0)

    def shared(msg, k, count, sem, i):
        part = msg.at[k, pl.ds(0, count - 1)]
        pltpu.make_async_copy(part, part, sem.at[i, k]).wait()

    def back_copies():
        left, right = {"col": col - 1}, {"col": col + 1}
        cor_near = remote(rows_of(acc_x, h_far), rows_of(back_x, h_far), bs, br, 0, {"row": near})
        cor_far = remote(rows_of(acc_x, h_near), rows_of(back_x, h_near), bs, br, 1, {"row": far})
        own_near = remote(rows_of(acc_r, h_far), rows_of(back_r, h_far), bs, br, 2, {"row": near})
        own_far = remote(rows_of(acc_r, h_near), rows_of(back_r, h_near), bs, br, 3, {"row": far})
        to_right = [remote(block_of(acc_c, h, 0), block_of(back_c, h, 0), bs, br, 4 + i, right)
                    for i, h in enumerate((h_near, h_far))]
        to_left = [remote(block_of(acc_c, h, half), block_of(back_c, h, half), bs, br, 6 + i, left)
                   for i, h in enumerate((h_near, h_far))]
        return cor_near, cor_far, own_near, own_far, to_right, to_left

    def iteration(k, carry):
        gather(lambda: pl.when(k == 0)(prepare))
        quad_ref[...] = jnp.zeros_like(quad_ref)
        lax.fori_loop(0, cap, forward, 0)
        scal_ref[2, 1:2, :] = quad_ref[...] + ridge_weight * scal_ref[2, 0:1, :]
        share(msg1, row, k, n_row, "row", row, 0)
        gather_done()
        acc_o[...] = ridge_weight * field[...]
        for ref in (acc_r, acc_c, acc_x):
            ref[...] = jnp.zeros_like(ref)
        lax.fori_loop(0, cap, inverse, 0)

        cor_near, cor_far, own_near, own_far, to_right, to_left = back_copies()
        cor_near.start()
        pl.when(has_far)(cor_far.start)
        own_near.start()
        pl.when(has_far)(own_far.start)
        shared(msg1, k, n_row, ar, 0)
        scal_ref[2] = jnp.sum(msg1[k], axis=0)
        share(msg2, col, k, n_col, "col", col, 1)
        cor_near.wait_recv()
        for i, h in ((0, h_near), (1, h_far)):
            if i == 1:
                pl.when(has_far)(cor_far.wait_recv)
            acc_c[:, pl.ds(h, half), :] += back_x[:, pl.ds(h, half), :]
            pl.when(has_right)(to_right[i].start)
            pl.when(has_left)(to_left[i].start)
        shared(msg2, k, n_col, ar, 1)
        total = jnp.sum(jnp.sum(msg2[k], axis=0), axis=1, keepdims=True)
        norm, product = total[0:1], total[1:2]
        before, alpha_before = scal_ref[0, 0:1, 0:1], scal_ref[1, 0:1, 0:1]
        ratio = jnp.where(k == 0, jnp.zeros_like(norm), norm / before)
        alpha = norm / (product - ratio * norm / alpha_before)
        scal_ref[0] = jnp.broadcast_to(norm, scal_ref.shape[1:])
        scal_ref[1] = jnp.broadcast_to(alpha, scal_ref.shape[1:])
        own_near.wait_recv()
        pl.when(has_far)(own_far.wait_recv)
        for i in (0, 1):
            pl.when(has_left)(to_right[i].wait_recv)
            pl.when(has_right)(to_left[i].wait_recv)
        image = acc_o[...] + back_r[...] + back_c[...]
        direction = field[...] + ratio[None] * d_ref[...]
        along = image + ratio[None] * along_ref[...]
        d_ref[...] = direction
        along_ref[...] = along
        x_ref[...] += alpha[None] * direction
        left_over = field[...] - alpha[None] * along
        field[...] = left_over
        scal_ref[2, 0:1, :] = lanes(jnp.sum(left_over * left_over, axis=(0, 1))[None])
        cor_near.wait_send()
        pl.when(has_far)(cor_far.wait_send)
        own_near.wait_send()
        pl.when(has_far)(own_far.wait_send)
        for i in (0, 1):
            pl.when(has_right)(to_right[i].wait_send)
            pl.when(has_left)(to_left[i].wait_send)
        shared(msg1, k, n_row, as_, 0)
        shared(msg2, k, n_col, as_, 1)
        return carry

    lax.fori_loop(0, ITERS, iteration, 0)
    x_out[...] = x_ref[...]
    r_out[...] = field[...]


def local(n_row, n_col, right_side, probe, detector_weights, offsets, counts):
    side, cap = probe.shape[1], offsets.shape[2]
    half = side // 2
    field = pltpu.VMEM((2, side, side), f32)
    vmem = pl.BlockSpec(memory_space=pltpu.VMEM)
    smem = pl.BlockSpec(memory_space=pltpu.SMEM)
    shape = jax.ShapeDtypeStruct(right_side.shape, f32)
    return pl.pallas_call(
        functools.partial(kernel, n_row, n_col, cap),
        out_shape=(shape, shape),
        in_specs=[vmem] * 4 + [smem] * 2,
        out_specs=(vmem, vmem),
        scratch_shapes=[field] * 11 + [
            pltpu.VMEM((cap, 2, side, side), f32),
            pltpu.VMEM((cap, 2, side, side), bf16),
            pltpu.VMEM((cap, 2, side, side), bf16),
            pltpu.VMEM((2, side, side), bf16),
            pltpu.VMEM((2, side, side), bf16),
            pltpu.VMEM((side, side), f32),
            field, field, field,
            pltpu.VMEM((1, half), f32),
            pltpu.VMEM((3, 2, half), f32),
            pltpu.VMEM((ITERS, n_row, 2, half), f32),
            pltpu.VMEM((ITERS, n_col, 2, half), f32),
            pltpu.SemaphoreType.DMA((8,)), pltpu.SemaphoreType.DMA((8,)),
            pltpu.SemaphoreType.DMA((8,)), pltpu.SemaphoreType.DMA((8,)),
            pltpu.SemaphoreType.DMA((2, ITERS)), pltpu.SemaphoreType.DMA((2, ITERS)),
        ],
        compiler_params=pltpu.CompilerParams(collective_id=0, has_side_effects=True),
    )(right_side, probe, detector_weights, jnp.asarray(tables(side)), offsets[0, 0], counts)


def solution(mesh):
    in_specs = (P(None, "row", "col"), P(), P(), P("row", "col", None, None), P("row", "col"))
    out_specs = (P(None, "row", "col"), P(None, "row", "col"))
    body = functools.partial(local, mesh.shape["row"], mesh.shape["col"])
    return jax.shard_map(body, mesh=mesh, in_specs=in_specs, out_specs=out_specs, check_vma=False)
```

profile of v0, /device:TPU:1, one launch (start us, length us, event | category | flops | bytes accessed | tf_op | source)
XLA Modules:
  0.0 105.4 jit_solution(4505429145459339419)
XLA Ops:
  1.3 0.0 copy-start.1
  1.3 0.7 copy-done.1
  2.0 0.7 copy.8.offs_ref
  2.6 100.0 %shard_map.77 = (f32[2,256,256]{2,1,0:T(8,128)}, f32[2,256,256]{2,1,0:T(8,128)}) custom-call(f32[2,256,256]{2,1,0:T(8,128)} %right_ref.1, f32[2,256,256]{2,1,0:T(8,128)} %probe_ref.1, f32[256,256]{1,0:T(8,128)} %weights_ref.1, bf16[8,256,256]{2,1,0:T(8,128)(2,1)} %constant.2.clone.mats_ref, s32[4,2]{1,0:T(4,128)} %copy.8.offs_ref, s32[1,1]{1,0:T(1,128)S(6)} %copy.11.count_ref), custom_call_target="tpu_custom_call" | custom-call | tf_op jit(solution)/shard_map/pallas_call | solution.py:341
  102.6 0.0 copy-start
  102.6 1.9 %copy.12 = f32[2,256,256]{2,1,0:T(8,128)} copy(f32[2,256,256]{2,1,0:T(8,128)} %get-tuple-element.4) | data formatting | bytes 1048576
  104.6 0.0 copy-done
  104.6 0.8 copy.13
Async XLA Ops:
  1.3 0.7 copy-start.1
  102.6 1.9 %copy-start = (f32[2,256,256]{2,1,0:T(8,128)S(1)}, f32[2,256,256]{2,1,0:T(8,128)}, u32[]{:S(2)}) copy-start(f32[2,256,256]{2,1,0:T(8,128)} %get-tuple-element.5) | copy-start | bytes 1572868
where the time goes:
time: 107 us; the launch traced here: 105 us
  Pallas kernels  100 us (93%)
  local copies, waits for them, and re-layouts  4.06 us (4%)
  between operations  1.3 us (1%)
    pallas_call x1, Pallas kernels, local(): pl.pallas_call(functools.partial(kernel, n_row, n_col, cap), out_shape=(s...  100 us
    unnamed x6, local copies, waits for them, and re-layouts  3.4 us

commit v1 on v0

v1 whole, which is shorter than its diff:
```python
import functools
import math

import jax
import jax.numpy as jnp
import numpy as np
from jax import lax
from jax.experimental import pallas as pl
from jax.experimental.pallas import tpu as pltpu
from jax.sharding import PartitionSpec as P

ITERS = 3
ridge_weight = 0.5
MESH = pl.DeviceIdType.MESH
f32 = jnp.float32
bf16 = jnp.bfloat16


def tables(side):
    half = side // 2
    n = np.arange(half)
    found = []
    for odd in (0, 1):
        phase = ((2 * np.arange(half) + odd)[:, None] * n[None, :]) % side
        angle = phase * (-2.0 * math.pi / side)
        re, im = np.cos(angle) / math.sqrt(side), np.sin(angle) / math.sqrt(side)
        found.append(np.block([[re, -im], [im, re]]).astype(np.float32))
    full = found + [mat.T.copy() for mat in found]
    out = []
    for mat in full:
        hi = mat.astype(jnp.bfloat16)
        out += [hi, (mat - hi.astype(np.float32)).astype(jnp.bfloat16)]
    return np.stack(out)


def split(value):
    hi = value.astype(bf16)
    return hi, (value - hi.astype(f32)).astype(bf16)


def dot(left, right):
    return jnp.dot(left, right, preferred_element_type=f32)


def kernel(n_row, n_col, cap, right_hbm, probe_hbm, weights_hbm, mats_hbm, offs_ref, count_ref,
           x_out, r_out,
           probe_ref, weights_ref, mats_ref, loads, field, halo_r, halo_c, halo_x, acc_o, acc_r, acc_c, acc_x, back_r, back_c, back_x,
           illum, spec_hi, spec_lo, wave_hi, wave_lo, wgt, x_ref, d_ref, along_ref,
           scal_ref, msg1, msg2, gs, gr, bs, br, as_, ar):
    side = field.shape[1]
    half = side // 2
    row, col = lax.axis_index("row"), lax.axis_index("col")
    odd = lax.rem(row, 2)
    near = row + 1 - 2 * odd
    far = row - 1 + 2 * odd
    has_far = jnp.logical_and(far >= 0, far < n_row)
    has_left, has_right = col > 0, col < n_col - 1
    h_far = pl.multiple_of(odd * half, half)
    h_near = pl.multiple_of(half - odd * half, half)

    fetch = [pltpu.make_async_copy(src, dst, loads.at[i]) for i, (src, dst) in enumerate((
        (right_hbm, field), (probe_hbm, probe_ref), (weights_hbm, weights_ref), (mats_hbm, mats_ref)))]
    for copy in fetch:
        copy.start()
    for ref in (halo_r, halo_c, halo_x, back_r, back_c, back_x):
        ref[...] = jnp.zeros_like(ref)

    barrier = pltpu.get_barrier_semaphore()

    def greet_row(step, carry):
        pl.semaphore_signal(barrier, inc=1, device_id={"row": lax.rem(row + step, n_row)}, device_id_type=MESH)
        return carry

    def greet_col(step, carry):
        pl.semaphore_signal(barrier, inc=1, device_id={"col": lax.rem(col + step, n_col)}, device_id_type=MESH)
        return carry

    lax.fori_loop(1, n_row, greet_row, 0)
    lax.fori_loop(1, n_col, greet_col, 0)
    for ref in (x_ref, d_ref, along_ref):
        ref[...] = jnp.zeros_like(ref)
    fetch[0].wait()
    pl.semaphore_wait(barrier, n_row + n_col - 2)

    def remote(src, dst, sems, rsems, i, target):
        return pltpu.make_async_remote_copy(
            src_ref=src, dst_ref=dst, send_sem=sems.at[i], recv_sem=rsems.at[i],
            device_id=target, device_id_type=MESH)

    quarter = half // 2

    def spans(first, second):
        return [pl.multiple_of(start + i * quarter, quarter) for start in (first, second) for i in (0, 1)]

    def rows_of(ref, start, count=half):
        return ref.at[:, pl.ds(start, count), :]

    def block_of(ref, start, col_start):
        return ref.at[:, pl.ds(start, quarter), pl.ds(col_start, half)]

    def gather_copies():
        left, right = {"col": col - 1}, {"col": col + 1}
        pieces = spans(h_far, h_near)
        to_left = [remote(block_of(field, h, 0), block_of(halo_c, h, 0), gs, gr, i, left)
                   for i, h in enumerate(pieces)]
        to_right = [remote(block_of(field, h, half), block_of(halo_c, h, half), gs, gr, 4 + i, right)
                    for i, h in enumerate(pieces)]
        own_far = remote(rows_of(field, h_far), rows_of(halo_r, h_far), gs, gr, 8, {"row": far})
        own_near = remote(rows_of(field, h_near), rows_of(halo_r, h_near), gs, gr, 9, {"row": near})
        corner = [remote(rows_of(halo_c, h, quarter), rows_of(halo_x, h, quarter), gs, gr, 10 + i,
                         {"row": far if i < 2 else near}) for i, h in enumerate(pieces)]
        return to_left, to_right, own_far, own_near, corner

    def if_far(i, action):
        if i < 2:
            pl.when(has_far)(action)
        else:
            action()

    def gather(between):
        to_left, to_right, own_far, own_near, corner = gather_copies()
        for i in range(4):
            pl.when(has_left)(to_left[i].start)
            pl.when(has_right)(to_right[i].start)
            if i == 0:
                pl.when(has_far)(own_far.start)
                own_near.start()
        between()
        for i in range(4):
            pl.when(has_right)(to_left[i].wait_recv)
            pl.when(has_left)(to_right[i].wait_recv)
            if_far(i, corner[i].start)
        pl.when(has_far)(own_far.wait_recv)
        own_near.wait_recv()
        for i in range(4):
            if_far(i, corner[i].wait_recv)

    def gather_done():
        to_left, to_right, own_far, own_near, corner = gather_copies()
        for i in range(4):
            pl.when(has_left)(to_left[i].wait_send)
            pl.when(has_right)(to_right[i].wait_send)
            if_far(i, corner[i].wait_send)
        pl.when(has_far)(own_far.wait_send)
        own_near.wait_send()

    def prepare():
        for copy in fetch[1:]:
            copy.wait()
        ramp_i = lax.broadcasted_iota(jnp.int32, (side, side), 0)
        ramp_j = lax.broadcasted_iota(jnp.int32, (side, side), 1)
        take = jnp.where(ramp_i < half, 2 * ramp_i, 2 * ramp_i + 1 - side)
        left = jnp.where(take == ramp_j, 1.0, 0.0).astype(f32)
        take_t = jnp.where(ramp_j < half, 2 * ramp_j, 2 * ramp_j + 1 - side)
        right = jnp.where(take_t == ramp_i, 1.0, 0.0).astype(f32)
        moved = jnp.dot(left, weights_ref[...], precision=lax.Precision.HIGHEST, preferred_element_type=f32)
        wgt[...] = jnp.dot(moved, right, precision=lax.Precision.HIGHEST, preferred_element_type=f32)

        def place(s, carry):
            down, across = offs_ref[0, s], offs_ref[1, s]
            down = jnp.where(down < 0, down + side, down)
            across = jnp.where(across < 0, across + side, across)
            flag = jnp.where(s < count_ref[0, 0], 1.0, 0.0).astype(f32)
            for part in (0, 1):
                rolled = pltpu.roll(probe_ref[part] * flag, down, 0)
                illum[s, part] = pltpu.roll(rolled, across, 1)
            return carry

        lax.fori_loop(0, cap, place, 0)
        scal_ref[0] = jnp.ones_like(scal_ref[0])
        scal_ref[1] = jnp.ones_like(scal_ref[1])
        first = field[...]
        scal_ref[2, 0:1, :] = lanes(jnp.sum(first * first, axis=(0, 1))[None])

    def lanes(value):
        return value[:, :half] + value[:, half:]

    def crosses(s, h):
        return s not in (0, 1) or s != h

    def row_mask(s, h):
        t = lax.broadcasted_iota(jnp.int32, (half, half), 0)
        return t >= offs_ref[0, s] if h == 0 else t < offs_ref[0, s] + half

    def col_mask(s, j):
        u = lax.broadcasted_iota(jnp.int32, (half, half), 1)
        return u >= offs_ref[1, s] if j == 0 else u < offs_ref[1, s] + half

    def span(h):
        return slice(h * half, (h + 1) * half)

    def stage_in(s, place):
        for h in (0, 1):
            wave = []
            for j in (0, 1):
                at = (span(h), span(j))
                view = []
                for part in (0, 1):
                    inner = field[part, *at]
                    if crosses(s, h):
                        inner = jnp.where(row_mask(s, h), inner, halo_r[part, *at])
                    if crosses(s, j):
                        outer = halo_c[part, *at]
                        if crosses(s, h):
                            outer = jnp.where(row_mask(s, h), outer, halo_x[part, *at])
                        inner = jnp.where(col_mask(s, j), inner, outer)
                    view.append(inner)
                pr, pi = illum[s, 0, *at], illum[s, 1, *at]
                wave.append((pr * view[0] - pi * view[1], pr * view[1] + pi * view[0]))
            rows = pl.ds(place * side + h * half, half)
            for which, sign in ((0, 1.0), (1, -1.0)):
                for part in (0, 1):
                    hi, lo = split(wave[0][part] + sign * wave[1][part])
                    wave_hi[which, rows, span(part)] = hi
                    wave_lo[which, rows, span(part)] = lo

    def across(mats, which, rows):
        return (dot(wave_hi[which, rows], mats_ref[mats]) + dot(wave_lo[which, rows], mats_ref[mats])
                + dot(wave_hi[which, rows], mats_ref[mats + 1]))

    def down(mats, hi, lo):
        return dot(mats_ref[mats], hi) + dot(mats_ref[mats + 1], hi) + dot(mats_ref[mats], lo)

    def forward(pair, base):
        for i, s in enumerate(pair):
            stage_in(s, base + i)
        rows = pl.ds(base * side, len(pair) * side)
        found = [across(4 + 2 * which, which, rows) for which in (0, 1)]
        quad = jnp.zeros((1, side), f32)
        for i, s in enumerate(pair):
            top, low = i * side, i * side + half
            for which, sign in ((0, 1.0), (1, -1.0)):
                both = [found[j][top:top + half] + sign * found[j][low:low + half] for j in (0, 1)]
                stacked = jnp.concatenate([
                    jnp.concatenate([both[0][:, :half], both[1][:, :half]], axis=1),
                    jnp.concatenate([both[0][:, half:], both[1][:, half:]], axis=1)], axis=0)
                freq = down(2 * which, *split(stacked))
                scale = wgt[span(which), :]
                scaled = freq * jnp.concatenate([scale, scale], axis=0)
                quad = quad + jnp.sum(freq * scaled, axis=0, keepdims=True)
                hi, lo = split(scaled)
                spec_hi[s, which] = hi
                spec_lo[s, which] = lo
        return quad

    def inverse(pair, base):
        for i, s in enumerate(pair):
            even = down(4, spec_hi[s, 0], spec_lo[s, 0])
            odd_ = down(6, spec_hi[s, 1], spec_lo[s, 1])
            for h, sign in ((0, 1.0), (1, -1.0)):
                both = even + sign * odd_
                rows = pl.ds((base + i) * side + h * half, half)
                for j in (0, 1):
                    for part in (0, 1):
                        hi, lo = split(both[span(part), span(j)])
                        wave_hi[j, rows, span(part)] = hi
                        wave_lo[j, rows, span(part)] = lo
        rows = pl.ds(base * side, len(pair) * side)
        out = [across(2 * j, j, rows) for j in (0, 1)]
        for i, s in enumerate(pair):
            for h in (0, 1):
                mine = slice(i * side + h * half, i * side + (h + 1) * half)
                for j, sign in ((0, 1.0), (1, -1.0)):
                    at = (span(h), span(j))
                    mixed = out[0][mine] + sign * out[1][mine]
                    hr, hi = mixed[:, :half], mixed[:, half:]
                    pr, pi = illum[s, 0, *at], illum[s, 1, *at]
                    for part, term in ((0, pr * hr + pi * hi), (1, pr * hi - pi * hr)):
                        scatter(s, h, j, part, term)

    def add_to(ref, s, first, part, at, value):
        if s == first:
            ref[part, *at] = value
        else:
            ref[part, *at] += value

    def scatter(s, h, j, part, term):
        at = (span(h), span(j))
        inner = term
        if crosses(s, h):
            inner = jnp.where(row_mask(s, h), term, 0.0)
            outer = term - inner
            if crosses(s, j):
                kept = jnp.where(col_mask(s, j), outer, 0.0)
                add_to(acc_x, s, min(t for t in range(cap) if crosses(t, h) and crosses(t, j)), part, at, outer - kept)
                outer = kept
            add_to(acc_r, s, min(t for t in range(cap) if crosses(t, h)), part, at, outer)
        if crosses(s, j):
            kept = jnp.where(col_mask(s, j), inner, 0.0)
            add_to(acc_c, s, min(t for t in range(cap) if crosses(t, j)), part, at, inner - kept)
            inner = kept
        if s == 0:
            inner = inner + ridge_weight * field[part, *at]
        add_to(acc_o, s, 0, part, at, inner)

    def share(msg, mine, k, count, axis, at, i):
        def send(step, carry):
            remote_to = {axis: lax.rem(mine + step, count)}
            pltpu.make_async_remote_copy(
                src_ref=msg.at[k, mine], dst_ref=msg.at[k, mine], send_sem=as_.at[i, k], recv_sem=ar.at[i, k],
                device_id=remote_to, device_id_type=MESH).start()
            return carry
        msg[k, at] = scal_ref[2]
        lax.fori_loop(1, count, send, 0)

    def shared(msg, k, count, sem, i):
        part = msg.at[k, pl.ds(0, count - 1)]
        pltpu.make_async_copy(part, part, sem.at[i, k]).wait()

    def back_copies():
        left, right = {"col": col - 1}, {"col": col + 1}
        out = spans(h_near, h_far)
        corner = [remote(rows_of(acc_x, h, quarter), rows_of(back_x, h, quarter), bs, br, i,
                         {"row": far if i < 2 else near}) for i, h in enumerate(out)]
        own_far = remote(rows_of(acc_r, h_near), rows_of(back_r, h_near), bs, br, 4, {"row": far})
        own_near = remote(rows_of(acc_r, h_far), rows_of(back_r, h_far), bs, br, 5, {"row": near})
        to_right = [remote(block_of(acc_c, h, 0), block_of(back_c, h, 0), bs, br, 6 + i, right)
                    for i, h in enumerate(out)]
        to_left = [remote(block_of(acc_c, h, half), block_of(back_c, h, half), bs, br, 10 + i, left)
                   for i, h in enumerate(out)]
        return corner, own_far, own_near, to_right, to_left, out

    def iteration(k, carry):
        gather(lambda: pl.when(k == 0)(prepare))
        pairs = [tuple(range(s, min(s + 2, cap))) for s in range(0, cap, 2)]
        quad = sum(forward(pair, pair[0]) for pair in pairs)
        scal_ref[2, 1:2, :] = lanes(quad) + ridge_weight * scal_ref[2, 0:1, :]
        share(msg1, col, k, n_col, "col", col, 0)
        gather_done()
        for pair in pairs:
            inverse(pair, pair[0])

        corner, own_far, own_near, to_right, to_left, out = back_copies()
        for i in range(4):
            if_far(i, corner[i].start)
        pl.when(has_far)(own_far.start)
        own_near.start()
        for i, h in enumerate(out):
            if_far((i + 2) % 4, corner[(i + 2) % 4].wait_recv)
            acc_c[:, pl.ds(h, quarter), :] += back_x[:, pl.ds(h, quarter), :]
            pl.when(has_right)(to_right[i].start)
            pl.when(has_left)(to_left[i].start)
            if i == 1:
                shared(msg1, k, n_col, ar, 0)
                scal_ref[2] = jnp.sum(msg1[k], axis=0)
                share(msg2, row, k, n_row, "row", row, 1)
        shared(msg2, k, n_row, ar, 1)
        total = jnp.sum(jnp.sum(msg2[k], axis=0), axis=1, keepdims=True)
        norm, product = total[0:1], total[1:2]
        before, alpha_before = scal_ref[0, 0:1, 0:1], scal_ref[1, 0:1, 0:1]
        ratio = jnp.where(k == 0, jnp.zeros_like(norm), norm / before)
        alpha = norm / (product - ratio * norm / alpha_before)
        scal_ref[0] = jnp.broadcast_to(norm, scal_ref.shape[1:])
        scal_ref[1] = jnp.broadcast_to(alpha, scal_ref.shape[1:])
        own_near.wait_recv()
        pl.when(has_far)(own_far.wait_recv)
        for i in range(4):
            pl.when(has_left)(to_right[i].wait_recv)
            pl.when(has_right)(to_left[i].wait_recv)
        image = acc_o[...] + back_r[...] + back_c[...]
        direction = field[...] + ratio[None] * d_ref[...]
        along = image + ratio[None] * along_ref[...]
        d_ref[...] = direction
        along_ref[...] = along
        x_ref[...] += alpha[None] * direction
        left_over = field[...] - alpha[None] * along
        field[...] = left_over
        scal_ref[2, 0:1, :] = lanes(jnp.sum(left_over * left_over, axis=(0, 1))[None])
        for i in range(4):
            if_far(i, corner[i].wait_send)
            pl.when(has_right)(to_right[i].wait_send)
            pl.when(has_left)(to_left[i].wait_send)
        own_near.wait_send()
        pl.when(has_far)(own_far.wait_send)
        shared(msg1, k, n_col, as_, 0)
        shared(msg2, k, n_row, as_, 1)
        return carry

    lax.fori_loop(0, ITERS, iteration, 0)
    x_out[...] = x_ref[...]
    r_out[...] = field[...]


def local(n_row, n_col, right_side, probe, detector_weights, offsets, counts):
    side, cap = probe.shape[1], offsets.shape[2]
    half = side // 2
    field = pltpu.VMEM((2, side, side), f32)
    vmem = pl.BlockSpec(memory_space=pltpu.VMEM)
    smem = pl.BlockSpec(memory_space=pltpu.SMEM)
    shape = pltpu.VMEM(right_side.shape, f32)
    return pl.pallas_call(
        functools.partial(kernel, n_row, n_col, cap),
        out_shape=(shape, shape),
        in_specs=[pl.BlockSpec(memory_space=pltpu.HBM)] * 4 + [smem] * 2,
        out_specs=(vmem, vmem),
        scratch_shapes=[
            field, pltpu.VMEM((side, side), f32), pltpu.VMEM((8, side, side), bf16), pltpu.SemaphoreType.DMA((4,)),
        ] + [field] * 11 + [
            pltpu.VMEM((cap, 2, side, side), f32),
            pltpu.VMEM((cap, 2, side, side), bf16),
            pltpu.VMEM((cap, 2, side, side), bf16),
            pltpu.VMEM((2, cap * side, side), bf16),
            pltpu.VMEM((2, cap * side, side), bf16),
            pltpu.VMEM((side, side), f32),
            field, field, field,
            pltpu.VMEM((3, 2, half), f32),
            pltpu.VMEM((ITERS, n_col, 2, half), f32),
            pltpu.VMEM((ITERS, n_row, 2, half), f32),
            pltpu.SemaphoreType.DMA((14,)), pltpu.SemaphoreType.DMA((14,)),
            pltpu.SemaphoreType.DMA((14,)), pltpu.SemaphoreType.DMA((14,)),
            pltpu.SemaphoreType.DMA((2, ITERS)), pltpu.SemaphoreType.DMA((2, ITERS)),
        ],
        compiler_params=pltpu.CompilerParams(collective_id=0, has_side_effects=True),
    )(right_side, probe, detector_weights, jnp.asarray(tables(side)), offsets[0, 0].T, counts)


def solution(mesh):
    in_specs = (P(None, "row", "col"), P(), P(), P("row", "col", None, None), P("row", "col"))
    out_specs = (P(None, "row", "col"), P(None, "row", "col"))
    body = functools.partial(local, mesh.shape["row"], mesh.shape["col"])
    return jax.shard_map(body, mesh=mesh, in_specs=in_specs, out_specs=out_specs, check_vma=False)
```

time: 107 us -> 93.7 us (0.88); the launches traced: 105 us -> 93.6 us
  Pallas kernels: 100 us -> 90.7 us
  local copies, waits for them, and re-layouts: 4.06 us -> 1.59 us
    pallas_call x1, Pallas kernels: 100 us -> 90.7 us  [local(): pl.pallas_call(functools.partial(kernel, n_row, n_col, cap), out_shape=(s...]
    unnamed x6 -> x2, local copies, waits for them, and re-layouts: 3.4 us -> 1.59 us
where the time goes in v1:
time: 93.7 us; the launch traced here: 93.6 us
  Pallas kernels  90.7 us (97%)
  local copies, waits for them, and re-layouts  1.59 us (2%)
  between operations  1.29 us (1%)
    pallas_call x1, Pallas kernels, local(): pl.pallas_call(functools.partial(kernel, n_row, n_col, cap), out_shape=(s...  90.7 us

profile of v1, /device:TPU:1, one launch (start us, length us, event | category | flops | bytes accessed | tf_op | source)
XLA Modules:
  0.0 93.6 jit_solution(3591484204690463174)
XLA Ops:
  1.3 90.7 %shard_map.77 = (f32[2,256,256]{2,1,0:T(8,128)S(1)}, f32[2,256,256]{2,1,0:T(8,128)S(1)}) custom-call(f32[2,256,256]{2,1,0:T(8,128)} %right_hbm.1, f32[2,256,256]{2,1,0:T(8,128)} %probe_hbm.1, f32[256,256]{1,0:T(8,128)} %weights_hbm.1, bf16[8,256,256]{2,1,0:T(8,128)(2,1)} %constant.2.clone.mats_hbm, s32[2,4]{1,0:T(2,128)} %bitcast.3, s32[1,1]{1,0:T(1,128)S(6)} %copy.12.count_ref), custom_call_target="tpu_custom_call" | custom-call | tf_op jit(solution)/shard_map/pallas_call | solution.py:391
  92.0 0.8 copy.10
  92.8 0.8 copy.11

commit v2 on v1

--- a/solution.py
+++ b/solution.py
@@ -42,9 +42,9 @@
     return jnp.dot(left, right, preferred_element_type=f32)
 
 
-def kernel(n_row, n_col, cap, right_hbm, probe_hbm, weights_hbm, mats_hbm, offs_ref, count_ref,
+def kernel(n_row, n_col, cap, right_hbm, probe_hbm, weights_hbm, mats_hbm, offs_hbm, count_hbm,
            x_out, r_out,
-           probe_ref, weights_ref, mats_ref, loads, field, halo_r, halo_c, halo_x, acc_o, acc_r, acc_c, acc_x, back_r, back_c, back_x,
+           probe_ref, weights_ref, mats_ref, offs_ref, count_ref, loads, field, halo_r, halo_c, halo_x, acc_o, acc_r, acc_c, acc_x, back_r, back_c, back_x,
            illum, spec_hi, spec_lo, wave_hi, wave_lo, wgt, x_ref, d_ref, along_ref,
            scal_ref, msg1, msg2, gs, gr, bs, br, as_, ar):
     side = field.shape[1]
@@ -59,7 +59,8 @@
     h_near = pl.multiple_of(half - odd * half, half)
 
     fetch = [pltpu.make_async_copy(src, dst, loads.at[i]) for i, (src, dst) in enumerate((
-        (right_hbm, field), (probe_hbm, probe_ref), (weights_hbm, weights_ref), (mats_hbm, mats_ref)))]
+        (right_hbm, field), (probe_hbm, probe_ref), (weights_hbm, weights_ref),
+        (mats_hbm, mats_ref), (offs_hbm, offs_ref), (count_hbm, count_ref)))]
     for copy in fetch:
         copy.start()
     for ref in (halo_r, halo_c, halo_x, back_r, back_c, back_x):
@@ -87,62 +88,80 @@
             src_ref=src, dst_ref=dst, send_sem=sems.at[i], recv_sem=rsems.at[i],
             device_id=target, device_id_type=MESH)
 
-    quarter = half // 2
-
-    def spans(first, second):
-        return [pl.multiple_of(start + i * quarter, quarter) for start in (first, second) for i in (0, 1)]
+    fine = half // 4
+    even_cut = [(i * fine, fine) for i in range(4)]
+    late_cut = [(0, 2 * fine), (2 * fine, fine), (3 * fine, fine)]
+    early_cut = [(0, fine), (fine, fine), (2 * fine, 2 * fine)]
+
+    def spans(*groups):
+        return [(pl.multiple_of(start + at, fine), size) for start, cut in groups for at, size in cut]
 
     def rows_of(ref, start, count=half):
         return ref.at[:, pl.ds(start, count), :]
 
-    def block_of(ref, start, col_start):
-        return ref.at[:, pl.ds(start, quarter), pl.ds(col_start, half)]
-
-    def gather_copies():
-        left, right = {"col": col - 1}, {"col": col + 1}
-        pieces = spans(h_far, h_near)
-        to_left = [remote(block_of(field, h, 0), block_of(halo_c, h, 0), gs, gr, i, left)
-                   for i, h in enumerate(pieces)]
-        to_right = [remote(block_of(field, h, half), block_of(halo_c, h, half), gs, gr, 4 + i, right)
-                    for i, h in enumerate(pieces)]
-        own_far = remote(rows_of(field, h_far), rows_of(halo_r, h_far), gs, gr, 8, {"row": far})
-        own_near = remote(rows_of(field, h_near), rows_of(halo_r, h_near), gs, gr, 9, {"row": near})
-        corner = [remote(rows_of(halo_c, h, quarter), rows_of(halo_x, h, quarter), gs, gr, 10 + i,
-                         {"row": far if i < 2 else near}) for i, h in enumerate(pieces)]
-        return to_left, to_right, own_far, own_near, corner
+    def block_of(ref, piece, col_start):
+        return ref.at[:, pl.ds(*piece), pl.ds(col_start, half)]
+
+    n_far = len(even_cut)
+    n_near = len(late_cut)
+    n_all = n_far + n_near
+    gather_pieces = spans((h_far, even_cut), (h_near, late_cut))
+    back_pieces = spans((h_near, early_cut), (h_far, even_cut))
+
+    left, right = {"col": col - 1}, {"col": col + 1}
+    to_left = [remote(block_of(field, h, 0), block_of(halo_c, h, 0), gs, gr, i, left)
+               for i, h in enumerate(gather_pieces)]
+    to_right = [remote(block_of(field, h, half), block_of(halo_c, h, half), gs, gr, n_all + i, right)
+                for i, h in enumerate(gather_pieces)]
+    own_far = remote(rows_of(field, h_far), rows_of(halo_r, h_far), gs, gr, 2 * n_all, {"row": far})
+    own_near = remote(rows_of(field, h_near), rows_of(halo_r, h_near), gs, gr, 2 * n_all + 1, {"row": near})
+    corner = [remote(rows_of(halo_c, *h), rows_of(halo_x, *h), gs, gr, 2 * n_all + 2 + i,
+                     {"row": far if i < n_far else near}) for i, h in enumerate(gather_pieces)]
 
     def if_far(i, action):
-        if i < 2:
+        if i < n_far:
             pl.when(has_far)(action)
         else:
             action()
 
-    def gather(between):
-        to_left, to_right, own_far, own_near, corner = gather_copies()
-        for i in range(4):
-            pl.when(has_left)(to_left[i].start)
-            pl.when(has_right)(to_right[i].start)
-            if i == 0:
-                pl.when(has_far)(own_far.start)
-                own_near.start()
-        between()
-        for i in range(4):
+    def send_piece(i, going):
+        pl.when(jnp.logical_and(going, has_left))(to_left[i].start)
+        pl.when(jnp.logical_and(going, has_right))(to_right[i].start)
+        if i == n_far - 1:
+            pl.when(jnp.logical_and(going, has_far))(own_far.start)
+        if i == n_all - 1:
+            pl.when(going)(own_near.start)
+
+    def gather():
+        for i in range(n_all):
             pl.when(has_right)(to_left[i].wait_recv)
             pl.when(has_left)(to_right[i].wait_recv)
             if_far(i, corner[i].start)
         pl.when(has_far)(own_far.wait_recv)
         own_near.wait_recv()
-        for i in range(4):
+        for i in range(n_all):
             if_far(i, corner[i].wait_recv)
 
     def gather_done():
-        to_left, to_right, own_far, own_near, corner = gather_copies()
-        for i in range(4):
+        for i in range(n_all):
             pl.when(has_left)(to_left[i].wait_send)
             pl.when(has_right)(to_right[i].wait_send)
             if_far(i, corner[i].wait_send)
         pl.when(has_far)(own_far.wait_send)
         own_near.wait_send()
+
+    far_out = spans((h_near, even_cut))
+    near_out = spans((h_far, early_cut))
+    back_far = [remote(rows_of(acc_x, *h), rows_of(back_x, *h), bs, br, i, {"row": far})
+                for i, h in enumerate(far_out)]
+    back_near = [remote(rows_of(acc_x, *h), rows_of(back_x, *h), bs, br, n_far + i, {"row": near})
+                 for i, h in enumerate(near_out)]
+    row_far = remote(rows_of(acc_r, h_near), rows_of(back_r, h_near), bs, br, n_all, {"row": far})
+    row_near = remote(rows_of(acc_r, h_far), rows_of(back_r, h_far), bs, br, n_all + 1, {"row": near})
+    col_right = [remote(block_of(acc_c, h, 0), block_of(back_c, h, 0), bs, br, n_all + 2 + i, right)
+                 for i, h in enumerate(back_pieces)]
+    col_left = [remote(block_of(acc_c, h, half), block_of(back_c, h, half), bs, br, 2 * n_all + 2 + i, left)
+                for i, h in enumerate(back_pieces)]
 
     def prepare():
         for copy in fetch[1:]:
@@ -307,21 +326,9 @@
         part = msg.at[k, pl.ds(0, count - 1)]
         pltpu.make_async_copy(part, part, sem.at[i, k]).wait()
 
-    def back_copies():
-        left, right = {"col": col - 1}, {"col": col + 1}
-        out = spans(h_near, h_far)
-        corner = [remote(rows_of(acc_x, h, quarter), rows_of(back_x, h, quarter), bs, br, i,
-                         {"row": far if i < 2 else near}) for i, h in enumerate(out)]
-        own_far = remote(rows_of(acc_r, h_near), rows_of(back_r, h_near), bs, br, 4, {"row": far})
-        own_near = remote(rows_of(acc_r, h_far), rows_of(back_r, h_far), bs, br, 5, {"row": near})
-        to_right = [remote(block_of(acc_c, h, 0), block_of(back_c, h, 0), bs, br, 6 + i, right)
-                    for i, h in enumerate(out)]
-        to_left = [remote(block_of(acc_c, h, half), block_of(back_c, h, half), bs, br, 10 + i, left)
-                   for i, h in enumerate(out)]
-        return corner, own_far, own_near, to_right, to_left, out
-
     def iteration(k, carry):
-        gather(lambda: pl.when(k == 0)(prepare))
+        pl.when(k == 0)(prepare)
+        gather()
         pairs = [tuple(range(s, min(s + 2, cap))) for s in range(0, cap, 2)]
         quad = sum(forward(pair, pair[0]) for pair in pairs)
         scal_ref[2, 1:2, :] = lanes(quad) + ridge_weight * scal_ref[2, 0:1, :]
@@ -330,52 +337,70 @@
         for pair in pairs:
             inverse(pair, pair[0])
 
-        corner, own_far, own_near, to_right, to_left, out = back_copies()
-        for i in range(4):
-            if_far(i, corner[i].start)
-        pl.when(has_far)(own_far.start)
-        own_near.start()
-        for i, h in enumerate(out):
-            if_far((i + 2) % 4, corner[(i + 2) % 4].wait_recv)
-            acc_c[:, pl.ds(h, quarter), :] += back_x[:, pl.ds(h, quarter), :]
-            pl.when(has_right)(to_right[i].start)
-            pl.when(has_left)(to_left[i].start)
-            if i == 1:
+        for copy in back_near:
+            copy.start()
+        for copy in back_far:
+            pl.when(has_far)(copy.start)
+        row_near.start()
+        for i, (start, size) in enumerate(back_pieces):
+            if i < n_near:
+                back_near[i].wait_recv()
+            else:
+                pl.when(has_far)(back_far[i - n_near].wait_recv)
+            acc_c[:, pl.ds(start, size), :] += back_x[:, pl.ds(start, size), :]
+            pl.when(has_right)(col_right[i].start)
+            pl.when(has_left)(col_left[i].start)
+            if i == n_near - 1:
                 shared(msg1, k, n_col, ar, 0)
                 scal_ref[2] = jnp.sum(msg1[k], axis=0)
                 share(msg2, row, k, n_row, "row", row, 1)
+                pl.when(has_far)(row_far.start)
         shared(msg2, k, n_row, ar, 1)
         total = jnp.sum(jnp.sum(msg2[k], axis=0), axis=1, keepdims=True)
         norm, product = total[0:1], total[1:2]
-        before, alpha_before = scal_ref[0, 0:1, 0:1], scal_ref[1, 0:1, 0:1]
-        ratio = jnp.where(k == 0, jnp.zeros_like(norm), norm / before)
+        norm_before, alpha_before = scal_ref[0, 0:1, 0:1], scal_ref[1, 0:1, 0:1]
+        ratio = jnp.where(k == 0, jnp.zeros_like(norm), norm / norm_before)
         alpha = norm / (product - ratio * norm / alpha_before)
         scal_ref[0] = jnp.broadcast_to(norm, scal_ref.shape[1:])
         scal_ref[1] = jnp.broadcast_to(alpha, scal_ref.shape[1:])
-        own_near.wait_recv()
-        pl.when(has_far)(own_far.wait_recv)
-        for i in range(4):
-            pl.when(has_left)(to_right[i].wait_recv)
-            pl.when(has_right)(to_left[i].wait_recv)
-        image = acc_o[...] + back_r[...] + back_c[...]
-        direction = field[...] + ratio[None] * d_ref[...]
-        along = image + ratio[None] * along_ref[...]
-        d_ref[...] = direction
-        along_ref[...] = along
-        x_ref[...] += alpha[None] * direction
-        left_over = field[...] - alpha[None] * along
-        field[...] = left_over
-        scal_ref[2, 0:1, :] = lanes(jnp.sum(left_over * left_over, axis=(0, 1))[None])
-        for i in range(4):
-            if_far(i, corner[i].wait_send)
-            pl.when(has_right)(to_right[i].wait_send)
-            pl.when(has_left)(to_left[i].wait_send)
-        own_near.wait_send()
-        pl.when(has_far)(own_far.wait_send)
+        row_near.wait_recv()
+        pl.when(has_far)(row_far.wait_recv)
+        for i in range(n_all):
+            pl.when(has_left)(col_right[i].wait_recv)
+            pl.when(has_right)(col_left[i].wait_recv)
+        square = jnp.zeros((1, side), f32)
+        going = k + 1 < ITERS
+        for i, (start, size) in enumerate(gather_pieces):
+            rows = pl.ds(start, size)
+            before = field[:, rows, :]
+            image = acc_o[:, rows, :] + back_r[:, rows, :] + back_c[:, rows, :]
+            direction = before + ratio[None] * d_ref[:, rows, :]
+            along = image + ratio[None] * along_ref[:, rows, :]
+            d_ref[:, rows, :] = direction
+            along_ref[:, rows, :] = along
+            x_ref[:, rows, :] += alpha[None] * direction
+            left_over = before - alpha[None] * along
+            field[:, rows, :] = left_over
+            square = square + jnp.sum(left_over * left_over, axis=(0, 1))[None]
+            if i > 0:
+                send_piece(i - 1, going)
+        send_piece(n_all - 1, going)
+        scal_ref[2, 0:1, :] = lanes(square)
+        for copy in back_near:
+            copy.wait_send()
+        for copy in back_far:
+            pl.when(has_far)(copy.wait_send)
+        row_near.wait_send()
+        pl.when(has_far)(row_far.wait_send)
+        for i in range(n_all):
+            pl.when(has_right)(col_right[i].wait_send)
+            pl.when(has_left)(col_left[i].wait_send)
         shared(msg1, k, n_col, as_, 0)
         shared(msg2, k, n_row, as_, 1)
         return carry
 
+    for i in range(n_all):
+        send_piece(i, True)
     lax.fori_loop(0, ITERS, iteration, 0)
     x_out[...] = x_ref[...]
     r_out[...] = field[...]
@@ -386,15 +411,15 @@
     half = side // 2
     field = pltpu.VMEM((2, side, side), f32)
     vmem = pl.BlockSpec(memory_space=pltpu.VMEM)
-    smem = pl.BlockSpec(memory_space=pltpu.SMEM)
     shape = pltpu.VMEM(right_side.shape, f32)
     return pl.pallas_call(
         functools.partial(kernel, n_row, n_col, cap),
         out_shape=(shape, shape),
-        in_specs=[pl.BlockSpec(memory_space=pltpu.HBM)] * 4 + [smem] * 2,
+        in_specs=[pl.BlockSpec(memory_space=pltpu.HBM)] * 6,
         out_specs=(vmem, vmem),
         scratch_shapes=[
-            field, pltpu.VMEM((side, side), f32), pltpu.VMEM((8, side, side), bf16), pltpu.SemaphoreType.DMA((4,)),
+            field, pltpu.VMEM((side, side), f32), pltpu.VMEM((8, side, side), bf16),
+            pltpu.SMEM((2, cap), jnp.int32), pltpu.SMEM((1, 1), jnp.int32), pltpu.SemaphoreType.DMA((6,)),
         ] + [field] * 11 + [
             pltpu.VMEM((cap, 2, side, side), f32),
             pltpu.VMEM((cap, 2, side, side), bf16),
@@ -406,8 +431,8 @@
             pltpu.VMEM((3, 2, half), f32),
             pltpu.VMEM((ITERS, n_col, 2, half), f32),
             pltpu.VMEM((ITERS, n_row, 2, half), f32),
-            pltpu.SemaphoreType.DMA((14,)), pltpu.SemaphoreType.DMA((14,)),
-            pltpu.SemaphoreType.DMA((14,)), pltpu.SemaphoreType.DMA((14,)),
+            pltpu.SemaphoreType.DMA((23,)), pltpu.SemaphoreType.DMA((23,)),
+            pltpu.SemaphoreType.DMA((23,)), pltpu.SemaphoreType.DMA((23,)),
             pltpu.SemaphoreType.DMA((2, ITERS)), pltpu.SemaphoreType.DMA((2, ITERS)),
         ],
         compiler_params=pltpu.CompilerParams(collective_id=0, has_side_effects=True),

time: 93.7 us -> 87.3 us (0.932); the launches traced: 93.6 us -> 86 us
  Pallas kernels: 90.7 us -> 83.1 us
    pallas_call x1, Pallas kernels: 90.7 us -> 83.1 us  [local(): pl.pallas_call(functools.partial(kernel, n_row, n_col, cap), out_shape=(s...]
where the time goes in v2:
time: 87.3 us; the launch traced here: 86 us
  Pallas kernels  83.1 us (95%)
  local copies, waits for them, and re-layouts  1.59 us (2%)
  between operations  1.29 us (1%)
    pallas_call x1, Pallas kernels, local(): pl.pallas_call(functools.partial(kernel, n_row, n_col, cap), out_shape=(s...  83.1 us

profile of v2, /device:TPU:1, one launch (start us, length us, event | category | flops | bytes accessed | tf_op | source)
XLA Modules:
  0.0 86.0 jit_solution(4307521716181612523)
XLA Ops:
  1.3 83.1 %shard_map.77 = (f32[2,256,256]{2,1,0:T(8,128)S(1)}, f32[2,256,256]{2,1,0:T(8,128)S(1)}) custom-call(f32[2,256,256]{2,1,0:T(8,128)} %right_hbm.1, f32[2,256,256]{2,1,0:T(8,128)} %probe_hbm.1, f32[256,256]{1,0:T(8,128)} %weights_hbm.1, bf16[8,256,256]{2,1,0:T(8,128)(2,1)} %constant.2.clone.mats_hbm, s32[2,4]{1,0:T(2,128)} %bitcast.3, s32[1,1]{1,0:T(1,128)S(6)} %copy.12.count_hbm), custom_call_target="tpu_custom_call" | custom-call | tf_op jit(solution)/shard_map/pallas_call | solution.py:415
  84.4 0.8 copy.10
  85.2 0.8 copy.11

commit v3 on v2

--- a/solution.py
+++ b/solution.py
@@ -30,7 +30,7 @@
     for mat in full:
         hi = mat.astype(jnp.bfloat16)
         out += [hi, (mat - hi.astype(np.float32)).astype(jnp.bfloat16)]
-    return np.stack(out)
+    return np.stack([np.stack([mat[:, :half], mat[:, half:]]) for mat in out])
 
 
 def split(value):
@@ -230,50 +230,62 @@
             for which, sign in ((0, 1.0), (1, -1.0)):
                 for part in (0, 1):
                     hi, lo = split(wave[0][part] + sign * wave[1][part])
-                    wave_hi[which, rows, span(part)] = hi
-                    wave_lo[which, rows, span(part)] = lo
+                    wave_hi[which, part, rows] = hi
+                    wave_lo[which, part, rows] = lo
+
+    def whole(ref, *at):
+        return jnp.concatenate([ref[*at[:1], j, *at[1:]] for j in (0, 1)], axis=1)
 
     def across(mats, which, rows):
-        return (dot(wave_hi[which, rows], mats_ref[mats]) + dot(wave_lo[which, rows], mats_ref[mats])
-                + dot(wave_hi[which, rows], mats_ref[mats + 1]))
-
-    def down(mats, hi, lo):
-        return dot(mats_ref[mats], hi) + dot(mats_ref[mats + 1], hi) + dot(mats_ref[mats], lo)
+        hi, lo = whole(wave_hi, which, rows), whole(wave_lo, which, rows)
+        fine_mat, rest = whole(mats_ref, mats), whole(mats_ref, mats + 1)
+        return dot(jnp.concatenate([hi, lo, hi], axis=1), jnp.concatenate([fine_mat, fine_mat, rest], axis=0))
+
+    def down(mats, s, which):
+        hi, lo = whole(spec_hi.at[s], which), whole(spec_lo.at[s], which)
+        fine_mat, rest = whole(mats_ref, mats), whole(mats_ref, mats + 1)
+        return dot(jnp.concatenate([fine_mat, rest, fine_mat], axis=1), jnp.concatenate([hi, hi, lo], axis=0))
+
+    def keep(s, which, j, part, value):
+        hi, lo = split(value)
+        spec_hi[s, which, j, span(part)] = hi
+        spec_lo[s, which, j, span(part)] = lo
 
     def forward(pair, base):
         for i, s in enumerate(pair):
             stage_in(s, base + i)
         rows = pl.ds(base * side, len(pair) * side)
         found = [across(4 + 2 * which, which, rows) for which in (0, 1)]
-        quad = jnp.zeros((1, side), f32)
+        quad = jnp.zeros((half, half), f32)
         for i, s in enumerate(pair):
             top, low = i * side, i * side + half
             for which, sign in ((0, 1.0), (1, -1.0)):
-                both = [found[j][top:top + half] + sign * found[j][low:low + half] for j in (0, 1)]
-                stacked = jnp.concatenate([
-                    jnp.concatenate([both[0][:, :half], both[1][:, :half]], axis=1),
-                    jnp.concatenate([both[0][:, half:], both[1][:, half:]], axis=1)], axis=0)
-                freq = down(2 * which, *split(stacked))
-                scale = wgt[span(which), :]
-                scaled = freq * jnp.concatenate([scale, scale], axis=0)
-                quad = quad + jnp.sum(freq * scaled, axis=0, keepdims=True)
-                hi, lo = split(scaled)
-                spec_hi[s, which] = hi
-                spec_lo[s, which] = lo
+                for j in (0, 1):
+                    both = found[j][top:top + half] + sign * found[j][low:low + half]
+                    for part in (0, 1):
+                        keep(s, which, j, part, both[:, span(part)])
+                freq = down(2 * which, s, which)
+                for j in (0, 1):
+                    scale = wgt[span(which), span(j)]
+                    for part in (0, 1):
+                        piece = freq[span(part), span(j)]
+                        scaled = piece * scale
+                        quad = quad + piece * scaled
+                        keep(s, which, j, part, scaled)
         return quad
 
     def inverse(pair, base):
         for i, s in enumerate(pair):
-            even = down(4, spec_hi[s, 0], spec_lo[s, 0])
-            odd_ = down(6, spec_hi[s, 1], spec_lo[s, 1])
+            even = down(4, s, 0)
+            odd_ = down(6, s, 1)
             for h, sign in ((0, 1.0), (1, -1.0)):
                 both = even + sign * odd_
                 rows = pl.ds((base + i) * side + h * half, half)
                 for j in (0, 1):
                     for part in (0, 1):
                         hi, lo = split(both[span(part), span(j)])
-                        wave_hi[j, rows, span(part)] = hi
-                        wave_lo[j, rows, span(part)] = lo
+                        wave_hi[j, part, rows] = hi
+                        wave_lo[j, part, rows] = lo
         rows = pl.ds(base * side, len(pair) * side)
         out = [across(2 * j, j, rows) for j in (0, 1)]
         for i, s in enumerate(pair):
@@ -329,9 +341,9 @@
     def iteration(k, carry):
         pl.when(k == 0)(prepare)
         gather()
-        pairs = [tuple(range(s, min(s + 2, cap))) for s in range(0, cap, 2)]
+        pairs = [tuple(range(cap))]
         quad = sum(forward(pair, pair[0]) for pair in pairs)
-        scal_ref[2, 1:2, :] = lanes(quad) + ridge_weight * scal_ref[2, 0:1, :]
+        scal_ref[2, 1:2, :] = jnp.sum(quad, axis=0, keepdims=True) + ridge_weight * scal_ref[2, 0:1, :]
         share(msg1, col, k, n_col, "col", col, 0)
         gather_done()
         for pair in pairs:
@@ -418,14 +430,14 @@
         in_specs=[pl.BlockSpec(memory_space=pltpu.HBM)] * 6,
         out_specs=(vmem, vmem),
         scratch_shapes=[
-            field, pltpu.VMEM((side, side), f32), pltpu.VMEM((8, side, side), bf16),
+            field, pltpu.VMEM((side, side), f32), pltpu.VMEM((8, 2, side, half), bf16),
             pltpu.SMEM((2, cap), jnp.int32), pltpu.SMEM((1, 1), jnp.int32), pltpu.SemaphoreType.DMA((6,)),
         ] + [field] * 11 + [
             pltpu.VMEM((cap, 2, side, side), f32),
-            pltpu.VMEM((cap, 2, side, side), bf16),
-            pltpu.VMEM((cap, 2, side, side), bf16),
-            pltpu.VMEM((2, cap * side, side), bf16),
-            pltpu.VMEM((2, cap * side, side), bf16),
+            pltpu.VMEM((cap, 2, 2, side, half), bf16),
+            pltpu.VMEM((cap, 2, 2, side, half), bf16),
+            pltpu.VMEM((2, 2, cap * side, half), bf16),
+            pltpu.VMEM((2, 2, cap * side, half), bf16),
             pltpu.VMEM((side, side), f32),
             field, field, field,
             pltpu.VMEM((3, 2, half), f32),

time: 87.3 us -> 85.6 us (0.981)
  Pallas kernels: 83.1 us -> 81.4 us
    pallas_call x1, Pallas kernels: 83.1 us -> 81.4 us  [local(): pl.pallas_call(functools.partial(kernel, n_row, n_col, cap), out_shape=(s...]
where the time goes in v3:
time: 85.6 us; the launch traced here: 84.3 us
  Pallas kernels  81.4 us (95%)
  local copies, waits for them, and re-layouts  1.59 us (2%)
  between operations  1.29 us (2%)
    pallas_call x1, Pallas kernels, local(): pl.pallas_call(functools.partial(kernel, n_row, n_col, cap), out_shape=(s...  81.4 us

profile of v3, /device:TPU:1, one launch (start us, length us, event | category | flops | bytes accessed | tf_op | source)
XLA Modules:
  0.0 84.3 jit_solution(3669894500217502714)
XLA Ops:
  1.3 81.4 %shard_map.77 = (f32[2,256,256]{2,1,0:T(8,128)S(1)}, f32[2,256,256]{2,1,0:T(8,128)S(1)}) custom-call(f32[2,256,256]{2,1,0:T(8,128)} %right_hbm.1, f32[2,256,256]{2,1,0:T(8,128)} %probe_hbm.1, f32[256,256]{1,0:T(8,128)} %weights_hbm.1, bf16[8,2,256,128]{3,2,1,0:T(8,128)(2,1)} %constant.2.clone.mats_hbm, s32[2,4]{1,0:T(2,128)} %bitcast.3, ...), custom_call_target="tpu_custom_call" | custom-call | tf_op jit(solution)/shard_map/pallas_call | solution.py:427
  82.7 0.8 copy.10
  83.5 0.8 copy.11

commit v4 on v3

v4 whole, which is shorter than its diff:
```python
import functools
import math

import jax
import jax.numpy as jnp
import numpy as np
from jax import lax
from jax.experimental import pallas as pl
from jax.experimental.pallas import tpu as pltpu
from jax.sharding import PartitionSpec as P

ITERS = 3
ridge_weight = 0.5
MESH = pl.DeviceIdType.MESH
f32 = jnp.float32
bf16 = jnp.bfloat16


def tables(side):
    half = side // 2
    n = np.arange(half)
    found = []
    for odd in (0, 1):
        phase = ((2 * np.arange(half) + odd)[:, None] * n[None, :]) % side
        angle = phase * (-2.0 * math.pi / side)
        re, im = np.cos(angle) / math.sqrt(side), np.sin(angle) / math.sqrt(side)
        found.append(np.block([[re, -im], [im, re]]).astype(np.float32))
    full = found + [mat.T.copy() for mat in found]
    out = []
    for mat in full:
        hi = mat.astype(jnp.bfloat16)
        out += [hi, (mat - hi.astype(np.float32)).astype(jnp.bfloat16)]
    return np.stack([np.stack([mat[:, :half], mat[:, half:]]) for mat in out])


def split(value):
    hi = value.astype(bf16)
    return hi, (value - hi.astype(f32)).astype(bf16)


def dot(left, right):
    return jnp.dot(left, right, preferred_element_type=f32)


def kernel(n_row, n_col, cap, right_hbm, probe_hbm, weights_hbm, mats_hbm, offs_hbm, count_hbm,
           both_out,
           probe_ref, weights_ref, mats_ref, offs_ref, count_ref, loads, field, halo_r, halo_c, halo_x, acc_o, acc_r, acc_c, acc_x, back_r, back_c, back_x,
           illum, spec_hi, spec_lo, duo_hi, duo_lo, wave_hi, wave_lo, gain_hi, gain_lo,
           early_ref, rest_ref, term_ref, wgt, x_ref, d_ref, along_ref,
           scal_ref, msg1, msg2, gs, gr, bs, br, as_, ar):
    side = field.shape[1]
    half = side // 2
    row, col = lax.axis_index("row"), lax.axis_index("col")
    odd = lax.rem(row, 2)
    near = row + 1 - 2 * odd
    far = row - 1 + 2 * odd
    has_far = jnp.logical_and(far >= 0, far < n_row)
    has_left, has_right = col > 0, col < n_col - 1
    h_far = pl.multiple_of(odd * half, half)
    h_near = pl.multiple_of(half - odd * half, half)

    fetch = [pltpu.make_async_copy(src, dst, loads.at[i]) for i, (src, dst) in enumerate((
        (right_hbm, field), (probe_hbm, probe_ref), (weights_hbm, weights_ref),
        (mats_hbm, mats_ref), (offs_hbm, offs_ref), (count_hbm, count_ref)))]
    for copy in fetch:
        copy.start()
    barrier = pltpu.get_barrier_semaphore()

    def far_first(count):
        return sorted(range(1, count), key=lambda step: -min(step, count - step))

    for step in far_first(n_col):
        pl.semaphore_signal(barrier, inc=1, device_id={"col": lax.rem(col + step, n_col)}, device_id_type=MESH)
    for step in far_first(n_row):
        pl.semaphore_signal(barrier, inc=1, device_id={"row": lax.rem(row + step, n_row)}, device_id_type=MESH)

    def clear(*views):
        def act():
            for view in views:
                view[...] = jnp.zeros(view.shape, f32)
        return act

    def band(ref, start):
        return ref.at[:, pl.ds(start, half), :]

    lower, upper = pl.ds(0, half), pl.ds(half, half)
    pl.when(jnp.logical_not(has_far))(clear(
        band(halo_r, h_near), band(halo_x, h_near), band(back_r, h_far), band(back_x, h_far)))
    pl.when(jnp.logical_not(has_left))(clear(halo_c.at[:, :, upper], back_c.at[:, :, lower]))
    pl.when(jnp.logical_not(has_right))(clear(halo_c.at[:, :, lower], back_c.at[:, :, upper]))
    for ref in (x_ref, d_ref, along_ref):
        ref[...] = jnp.zeros_like(ref)
    fetch[0].wait()
    pl.semaphore_wait(barrier, n_row + n_col - 2)

    def remote(src, dst, sems, rsems, i, target):
        return pltpu.make_async_remote_copy(
            src_ref=src, dst_ref=dst, send_sem=sems.at[i], recv_sem=rsems.at[i],
            device_id=target, device_id_type=MESH)

    fine = half // 4
    even_cut = [(i * fine, fine) for i in range(4)]
    late_cut = [(0, 2 * fine), (2 * fine, fine), (3 * fine, fine)]
    early_cut = [(0, fine), (fine, fine), (2 * fine, 2 * fine)]

    def spans(*groups):
        return [(pl.multiple_of(start + at, fine), size) for start, cut in groups for at, size in cut]

    def rows_of(ref, start, count=half):
        return ref.at[:, pl.ds(start, count), :]

    def block_of(ref, piece, col_start):
        return ref.at[:, pl.ds(*piece), pl.ds(col_start, half)]

    n_far = len(even_cut)
    n_near = len(late_cut)
    n_all = n_far + n_near
    gather_pieces = spans((h_far, even_cut), (h_near, late_cut))
    back_pieces = spans((h_near, early_cut), (h_far, even_cut))

    left, right = {"col": col - 1}, {"col": col + 1}
    to_left = [remote(block_of(field, h, 0), block_of(halo_c, h, 0), gs, gr, i, left)
               for i, h in enumerate(gather_pieces)]
    to_right = [remote(block_of(field, h, half), block_of(halo_c, h, half), gs, gr, n_all + i, right)
                for i, h in enumerate(gather_pieces)]
    own_far = remote(rows_of(field, h_far), rows_of(halo_r, h_far), gs, gr, 2 * n_all, {"row": far})
    own_near = remote(rows_of(field, h_near), rows_of(halo_r, h_near), gs, gr, 2 * n_all + 1, {"row": near})
    corner = [remote(rows_of(halo_c, *h), rows_of(halo_x, *h), gs, gr, 2 * n_all + 2 + i,
                     {"row": far if i < n_far else near}) for i, h in enumerate(gather_pieces)]

    def if_far(i, action):
        if i < n_far:
            pl.when(has_far)(action)
        else:
            action()

    def send_piece(i, going):
        pl.when(jnp.logical_and(going, has_left))(to_left[i].start)
        pl.when(jnp.logical_and(going, has_right))(to_right[i].start)
        if i == n_far - 1:
            pl.when(jnp.logical_and(going, has_far))(own_far.start)
        if i == n_all - 1:
            pl.when(going)(own_near.start)

    def advance():
        x_ref[...] += scal_ref[1, 0:1, 0:1][None] * d_ref[...]

    def gather():
        def pass_on(i):
            pl.when(has_right)(to_left[i].wait_recv)
            pl.when(has_left)(to_right[i].wait_recv)
            if_far(i, corner[i].start)

        for i in range(n_far):
            pass_on(i)
        own_near.wait_recv()
        pl.when(has_far)(own_far.wait_recv)
        advance()
        early(range(cap // 2))
        for i in range(n_far, n_all):
            pass_on(i)
        early(range(cap // 2, cap))
        for i in range(n_all):
            if_far(i, corner[i].wait_recv)

    def gather_done():
        for i in range(n_all):
            pl.when(has_left)(to_left[i].wait_send)
            pl.when(has_right)(to_right[i].wait_send)
            if_far(i, corner[i].wait_send)
        pl.when(has_far)(own_far.wait_send)
        own_near.wait_send()

    far_out = spans((h_near, even_cut))
    near_out = spans((h_far, early_cut))
    back_far = [remote(rows_of(acc_x, *h), rows_of(back_x, *h), bs, br, i, {"row": far})
                for i, h in enumerate(far_out)]
    back_near = [remote(rows_of(acc_x, *h), rows_of(back_x, *h), bs, br, n_far + i, {"row": near})
                 for i, h in enumerate(near_out)]
    row_far = [remote(rows_of(acc_r, start, 2 * fine), rows_of(back_r, start, 2 * fine), bs, br, at, {"row": far})
               for at, (start, _) in zip((n_all, 3 * n_all + 2), (far_out[0], far_out[2]))]
    row_near = remote(rows_of(acc_r, h_far), rows_of(back_r, h_far), bs, br, n_all + 1, {"row": near})
    col_right = [remote(block_of(acc_c, h, 0), block_of(back_c, h, 0), bs, br, n_all + 2 + i, right)
                 for i, h in enumerate(back_pieces)]
    col_left = [remote(block_of(acc_c, h, half), block_of(back_c, h, half), bs, br, 2 * n_all + 2 + i, left)
                for i, h in enumerate(back_pieces)]

    def prepare():
        for copy in fetch[1:]:
            copy.wait()
        ramp_i = lax.broadcasted_iota(jnp.int32, (side, side), 0)
        ramp_j = lax.broadcasted_iota(jnp.int32, (side, side), 1)
        take = jnp.where(ramp_i < half, 2 * ramp_i, 2 * ramp_i + 1 - side)
        left = jnp.where(take == ramp_j, 1.0, 0.0).astype(f32)
        take_t = jnp.where(ramp_j < half, 2 * ramp_j, 2 * ramp_j + 1 - side)
        right = jnp.where(take_t == ramp_i, 1.0, 0.0).astype(f32)
        moved = jnp.dot(left, weights_ref[...], precision=lax.Precision.HIGHEST, preferred_element_type=f32)
        wgt[...] = jnp.dot(moved, right, precision=lax.Precision.HIGHEST, preferred_element_type=f32)

        def place(s, carry):
            down, across = offs_ref[0, s], offs_ref[1, s]
            down = jnp.where(down < 0, down + side, down)
            across = jnp.where(across < 0, across + side, across)
            flag = jnp.where(s < count_ref[0, 0], 1.0, 0.0).astype(f32)
            flipped = turned(s, side)
            for part in (0, 1):
                rolled = pltpu.roll(probe_ref[part] * flag, down, 0)
                rolled = pltpu.roll(rolled, across, 1)
                lower, upper = rolled[:, :half], rolled[:, half:]
                illum[s, 0, part] = jnp.where(flipped, upper, lower)
                illum[s, 1, part] = jnp.where(flipped, lower, upper)
            return carry

        lax.fori_loop(0, cap, place, 0)
        scal_ref[0] = jnp.ones_like(scal_ref[0])
        scal_ref[1] = jnp.ones_like(scal_ref[1])
        first = field[...]
        scal_ref[2, 0:1, :] = lanes(jnp.sum(first * first, axis=(0, 1))[None])

    def lanes(value):
        return value[:, :half] + value[:, half:]

    def crosses(s, h):
        return s not in (0, 1) or s != h

    def span(h):
        return slice(h * half, (h + 1) * half)

    def row_mask(s, h):
        t = lax.broadcasted_iota(jnp.int32, (half, half), 0)
        return t >= offs_ref[0, s] if h == 0 else t < offs_ref[0, s] + half

    def turned(s, rows=half):
        return jnp.broadcast_to(offs_ref[1, s], (rows, half)) < 0

    def crossing(s, turn, ref, part, h):
        first, second = ref.at[part, span(h), span(0)], ref.at[part, span(h), span(1)]
        if s in (0, 1):
            return (second if s == turn else first)[...]
        if turn == 0:
            return jnp.where(turned(s), second[...], first[...])
        return jnp.where(turned(s), first[...], second[...])

    def own_columns(s):
        u = lax.broadcasted_iota(jnp.int32, (half, half), 1)
        shift = offs_ref[1, s]
        if s == 0:
            return u < shift + half
        if s == 1:
            return u >= shift
        sign = jnp.where(shift < 0, -1, 1)
        return u * sign >= jnp.where(shift < 0, 1 - half - shift, shift)

    def by_column(s, first, second):
        if s == 0:
            return second, first
        if s == 1:
            return first, second
        return jnp.where(turned(s), second, first), jnp.where(turned(s), first, second)

    def lit(s, turn, rows, view):
        pr, pi = illum[s, turn, 0, rows], illum[s, turn, 1, rows]
        return pr * view[0] - pi * view[1], pr * view[1] + pi * view[0]

    def whole(ref, *at):
        return jnp.concatenate([ref[*at, j] for j in (0, 1)], axis=1)

    def triple(ref, at):
        main, rest = whole(ref, at), whole(ref, at + 1)
        return main, rest

    def across(mats, hi_ref, lo_ref, which):
        hi, lo = whole(hi_ref, which), whole(lo_ref, which)
        main, rest = triple(mats_ref, mats)
        return dot(jnp.concatenate([hi, lo, hi], axis=1), jnp.concatenate([main, main, rest], axis=0))

    def down(mats, hi_ref, lo_ref, *at):
        hi, lo = whole(hi_ref, *at), whole(lo_ref, *at)
        main, rest = triple(mats_ref, mats)
        return dot(jnp.concatenate([main, rest, main], axis=1), jnp.concatenate([hi, hi, lo], axis=0))

    def keep(hi_ref, lo_ref, at, value):
        hi, lo = split(value)
        hi_ref[*at] = hi
        lo_ref[*at] = lo

    def early(slots):
        for s in slots:
            own = own_columns(s)
            for turn in (0, 1):
                wave = []
                for h in (0, 1):
                    view = []
                    for part in (0, 1):
                        value = crossing(s, turn, field, part, h)
                        if crosses(s, h):
                            value = jnp.where(row_mask(s, h), value, crossing(s, turn, halo_r, part, h))
                        if turn == 0:
                            value = jnp.where(own, value, 0.0)
                        view.append(value)
                    wave.append(lit(s, turn, span(h), view))
                for which, sign in ((0, 1.0), (1, -1.0)):
                    for part in (0, 1):
                        keep(spec_hi, spec_lo, (s, which, turn, span(part)), wave[0][part] + sign * wave[1][part])
        for s in slots:
            for which in (0, 1):
                found = down(2 * which, spec_hi, spec_lo, s, which)
                first, second = found[:, :half], found[:, half:]
                early_ref[s, 0, which] = first + second
                early_ref[s, 1, which] = first - second

    def late():
        for s in range(cap):
            own = own_columns(s)
            wave = []
            for h in (0, 1):
                view = []
                for part in (0, 1):
                    value = crossing(s, 0, halo_c, part, h)
                    if crosses(s, h):
                        value = jnp.where(row_mask(s, h), value, crossing(s, 0, halo_x, part, h))
                    view.append(jnp.where(own, 0.0, value))
                wave.append(lit(s, 0, span(h), view))
            for which, sign in ((0, 1.0), (1, -1.0)):
                for part in (0, 1):
                    keep(duo_hi, duo_lo, (0, s // 2, which, s % 2, span(part)), wave[0][part] + sign * wave[1][part])
        for pair in range(cap // 2):
            for which in (0, 1):
                found = down(2 * which, duo_hi, duo_lo, 0, pair, which)
                for i in (0, 1):
                    s = 2 * pair + i
                    rows = pl.ds(s * side + which * half, half)
                    for odd_col in (0, 1):
                        total = early_ref[s, odd_col, which] + found[:, span(i)]
                        for part in (0, 1):
                            keep(wave_hi, wave_lo, (odd_col, part, rows), total[span(part)])
        quad = jnp.zeros((side, half), f32)
        for odd_col in (0, 1):
            found = across(4 + 2 * odd_col, wave_hi, wave_lo, odd_col)
            for s in range(cap):
                rows = slice(s * side, (s + 1) * side)
                scale = wgt[:, span(odd_col)]
                for part in (0, 1):
                    piece = found[rows, span(part)]
                    scaled = piece * scale
                    quad = quad + piece * scaled
                    keep(gain_hi, gain_lo, (odd_col, part, pl.ds(s * side, side)), scaled)
        return jnp.sum(quad, axis=0, keepdims=True)

    def add_to(ref, first, part, at, value):
        if first:
            ref[part, *at] = value
        else:
            ref[part, *at] += value

    def terms(s, turn, h, i, even, odd_row):
        both = even[:, span(i)] + odd_row[:, span(i)] if h == 0 else even[:, span(i)] - odd_row[:, span(i)]
        hr, hi = both[:half], both[half:]
        pr, pi = illum[s, turn, 0, span(h)], illum[s, turn, 1, span(h)]
        return pr * hr + pi * hi, pr * hi - pi * hr

    def inverse_crossing():
        found = [across(2 * odd_col, gain_hi, gain_lo, odd_col) for odd_col in (0, 1)]
        for s in range(cap):
            for which in (0, 1):
                rows = slice(s * side + which * half, s * side + (which + 1) * half)
                first, second = found[0][rows] + found[1][rows], found[0][rows] - found[1][rows]
                rest_ref[s, which] = second
                for part in (0, 1):
                    keep(duo_hi, duo_lo, (1, s // 2, which, s % 2, span(part)), first[:, span(part)])
        for pair in range(cap // 2):
            even = down(4, duo_hi, duo_lo, 1, pair, 0)
            odd_row = down(6, duo_hi, duo_lo, 1, pair, 1)
            for i in (0, 1):
                s = 2 * pair + i
                own = own_columns(s)
                for h in (0, 1):
                    for part, term in enumerate(terms(s, 0, h, i, even, odd_row)):
                        term_ref[s, part, span(h)] = term
                        beyond = jnp.where(own, 0.0, term)
                        inner = beyond
                        if crosses(s, h):
                            inner = jnp.where(row_mask(s, h), beyond, 0.0)
                            spread(acc_x, s, h, part, beyond - inner, True)
                        spread(acc_c, s, h, part, inner, False)

    def spread(ref, s, h, part, value, corner_only):
        def first(j):
            able = [t for t in range(cap) if (t > 1 or t != j) and (crosses(t, h) or not corner_only)]
            return s == min(able)
        if s in (0, 1):
            add_to(ref, first(1 - s), part, (span(h), span(1 - s)), value)
        else:
            near_half = jnp.where(turned(s), 0.0, value)
            add_to(ref, first(0), part, (span(h), span(0)), near_half)
            add_to(ref, first(1), part, (span(h), span(1)), value - near_half)

    def inverse_rest():
        for s in range(cap):
            for which in (0, 1):
                for part in (0, 1):
                    keep(duo_hi, duo_lo, (2, s // 2, which, s % 2, span(part)), rest_ref[s, which, :, span(part)])
        for pair in range(cap // 2):
            even = down(4, duo_hi, duo_lo, 2, pair, 0)
            odd_row = down(6, duo_hi, duo_lo, 2, pair, 1)
            for i in (0, 1):
                s = 2 * pair + i
                own = own_columns(s)
                for h in (0, 1):
                    for part, term in enumerate(terms(s, 1, h, i, even, odd_row)):
                        crossed = jnp.where(own, term_ref[s, part, span(h)], 0.0)
                        for j, value in enumerate(by_column(s, crossed, term)):
                            at = (span(h), span(j))
                            inner = value
                            if crosses(s, h):
                                inner = jnp.where(row_mask(s, h), value, 0.0)
                                add_to(acc_r, s == min(t for t in range(cap) if crosses(t, h)), part, at, value - inner)
                            if s == 0:
                                inner = inner + ridge_weight * field[part, *at]
                            add_to(acc_o, s == 0, part, at, inner)

    def share(msg, mine, k, count, axis, at, i):
        def send(step, carry):
            remote_to = {axis: lax.rem(mine + step, count)}
            pltpu.make_async_remote_copy(
                src_ref=msg.at[k, mine], dst_ref=msg.at[k, mine], send_sem=as_.at[i, k], recv_sem=ar.at[i, k],
                device_id=remote_to, device_id_type=MESH).start()
            return carry
        msg[k, at] = scal_ref[2]
        lax.fori_loop(1, count, send, 0)

    def shared(msg, k, count, sem, i):
        part = msg.at[k, pl.ds(0, count - 1)]
        pltpu.make_async_copy(part, part, sem.at[i, k]).wait()

    def iteration(k, carry):
        pl.when(k == 0)(prepare)
        gather()
        quad = late()
        scal_ref[2, 1:2, :] = quad + ridge_weight * scal_ref[2, 0:1, :]
        share(msg1, col, k, n_col, "col", col, 0)
        gather_done()
        inverse_crossing()
        for copy in back_near:
            copy.start()
        for copy in back_far:
            pl.when(has_far)(copy.start)
        inverse_rest()
        row_near.start()
        pl.when(has_far)(row_far[0].start)
        for i, (start, size) in enumerate(back_pieces):
            if i < n_near:
                back_near[i].wait_recv()
            else:
                pl.when(has_far)(back_far[i - n_near].wait_recv)
            acc_c[:, pl.ds(start, size), :] += back_x[:, pl.ds(start, size), :]
            pl.when(has_right)(col_right[i].start)
            pl.when(has_left)(col_left[i].start)
            if i == n_near - 1:
                shared(msg1, k, n_col, ar, 0)
                scal_ref[2] = jnp.sum(msg1[k], axis=0)
                share(msg2, row, k, n_row, "row", row, 1)
                pl.when(has_far)(row_far[1].start)
        shared(msg2, k, n_row, ar, 1)
        total = jnp.sum(jnp.sum(msg2[k], axis=0), axis=1, keepdims=True)
        norm, product = total[0:1], total[1:2]
        norm_before, alpha_before = scal_ref[0, 0:1, 0:1], scal_ref[1, 0:1, 0:1]
        ratio = jnp.where(k == 0, jnp.zeros_like(norm), norm / norm_before)
        alpha = norm / (product - ratio * norm / alpha_before)
        scal_ref[0] = jnp.broadcast_to(norm, scal_ref.shape[1:])
        scal_ref[1] = jnp.broadcast_to(alpha, scal_ref.shape[1:])
        row_near.wait_recv()
        for copy in row_far:
            pl.when(has_far)(copy.wait_recv)
        for i in range(n_all):
            pl.when(has_left)(col_right[i].wait_recv)
            pl.when(has_right)(col_left[i].wait_recv)
        square = jnp.zeros((1, side), f32)
        going = k + 1 < ITERS
        for i, (start, size) in enumerate(gather_pieces):
            rows = pl.ds(start, size)
            before = field[:, rows, :]
            image = acc_o[:, rows, :] + back_r[:, rows, :] + back_c[:, rows, :]
            direction = before + ratio[None] * d_ref[:, rows, :]
            along = image + ratio[None] * along_ref[:, rows, :]
            d_ref[:, rows, :] = direction
            along_ref[:, rows, :] = along
            left_over = before - alpha[None] * along
            field[:, rows, :] = left_over
            square = square + jnp.sum(left_over * left_over, axis=(0, 1))[None]
            if i > 0:
                send_piece(i - 1, going)
        send_piece(n_all - 1, going)
        scal_ref[2, 0:1, :] = lanes(square)
        for copy in back_near:
            copy.wait_send()
        for copy in back_far:
            pl.when(has_far)(copy.wait_send)
        row_near.wait_send()
        for copy in row_far:
            pl.when(has_far)(copy.wait_send)
        for i in range(n_all):
            pl.when(has_right)(col_right[i].wait_send)
            pl.when(has_left)(col_left[i].wait_send)
        shared(msg1, k, n_col, as_, 0)
        shared(msg2, k, n_row, as_, 1)
        return carry

    for i in range(n_all):
        send_piece(i, True)
    lax.fori_loop(0, ITERS, iteration, 0)
    both_out[0] = x_ref[...] + scal_ref[1, 0:1, 0:1][None] * d_ref[...]
    both_out[1] = field[...]


def local(n_row, n_col, right_side, probe, detector_weights, offsets, counts):
    side, cap = probe.shape[1], offsets.shape[2]
    half = side // 2
    field = pltpu.VMEM((2, side, side), f32)
    vmem = pl.BlockSpec(memory_space=pltpu.VMEM)
    both = pl.pallas_call(
        functools.partial(kernel, n_row, n_col, cap),
        out_shape=pltpu.VMEM((2,) + right_side.shape, f32),
        in_specs=[pl.BlockSpec(memory_space=pltpu.HBM)] * 6,
        out_specs=vmem,
        scratch_shapes=[
            field, pltpu.VMEM((side, side), f32), pltpu.VMEM((8, 2, side, half), bf16),
            pltpu.SMEM((2, cap), jnp.int32), pltpu.SMEM((1, 1), jnp.int32), pltpu.SemaphoreType.DMA((6,)),
        ] + [field] * 11 + [
            pltpu.VMEM((cap, 2, 2, side, half), f32),
            pltpu.VMEM((cap, 2, 2, side, half), bf16),
            pltpu.VMEM((cap, 2, 2, side, half), bf16),
            pltpu.VMEM((3, cap // 2, 2, 2, side, half), bf16),
            pltpu.VMEM((3, cap // 2, 2, 2, side, half), bf16),
            pltpu.VMEM((2, 2, cap * side, half), bf16),
            pltpu.VMEM((2, 2, cap * side, half), bf16),
            pltpu.VMEM((2, 2, cap * side, half), bf16),
            pltpu.VMEM((2, 2, cap * side, half), bf16),
            pltpu.VMEM((cap, 2, 2, side, half), f32),
            pltpu.VMEM((cap, 2, half, side), f32),
            pltpu.VMEM((cap, 2, side, half), f32),
            pltpu.VMEM((side, side), f32),
            field, field, field,
            pltpu.VMEM((3, 2, half), f32),
            pltpu.VMEM((ITERS, n_col, 2, half), f32),
            pltpu.VMEM((ITERS, n_row, 2, half), f32),
            pltpu.SemaphoreType.DMA((24,)), pltpu.SemaphoreType.DMA((24,)),
            pltpu.SemaphoreType.DMA((24,)), pltpu.SemaphoreType.DMA((24,)),
            pltpu.SemaphoreType.DMA((2, ITERS)), pltpu.SemaphoreType.DMA((2, ITERS)),
        ],
        compiler_params=pltpu.CompilerParams(collective_id=0, has_side_effects=True),
    )(right_side, probe, detector_weights, jnp.asarray(tables(side)), offsets[0, 0].T, counts)
    return both[0], both[1]


def solution(mesh):
    in_specs = (P(None, "row", "col"), P(), P(), P("row", "col", None, None), P("row", "col"))
    out_specs = (P(None, "row", "col"), P(None, "row", "col"))
    body = functools.partial(local, mesh.shape["row"], mesh.shape["col"])
    return jax.shard_map(body, mesh=mesh, in_specs=in_specs, out_specs=out_specs, check_vma=False)
```

time: 85.6 us -> 82 us (0.958); the launches traced: 84.3 us -> 81.9 us
  Pallas kernels: 81.4 us -> 79.5 us
    pallas_call x1, Pallas kernels: 81.4 us -> 79.5 us  [local(): pl.pallas_call(functools.partial(kernel, n_row, n_col, cap), out_shape=pl...]
    unnamed x2 -> x0, local copies, waits for them, and re-layouts: 1.59 us -> none
    squeeze x0 -> x1, local copies, waits for them, and re-layouts: none -> 1.03 us  [local(): return (both[0], both[1])]
where the time goes in v4:
time: 82 us; the launch traced here: 81.9 us
  Pallas kernels  79.5 us (97%)
  between operations  1.29 us (2%)
  local copies, waits for them, and re-layouts  1.03 us (1%)
    pallas_call x1, Pallas kernels, local(): pl.pallas_call(functools.partial(kernel, n_row, n_col, cap), out_shape=pl...  79.5 us

profile of v4, /device:TPU:1, one launch (start us, length us, event | category | flops | bytes accessed | tf_op | source)
XLA Modules:
  0.0 81.9 jit_solution(5661801845401892723)
XLA Ops:
  1.3 79.5 %shard_map.77 = f32[2,2,256,256]{3,2,1,0:T(8,128)S(1)} custom-call(f32[2,256,256]{2,1,0:T(8,128)} %right_hbm.1, f32[2,256,256]{2,1,0:T(8,128)} %probe_hbm.1, f32[256,256]{1,0:T(8,128)} %weights_hbm.1, bf16[8,2,256,128]{3,2,1,0:T(8,128)(2,1)} %constant.2.clone.mats_hbm, s32[2,4]{1,0:T(2,128)} %bitcast.7, s32[1,1]{1,0:T(1,128)S(6)} %copy.8.count_hbm), custom_call_target="tpu_custom_call" | custom-call | tf_op jit(solution)/shard_map/pallas_call | solution.py:521
  80.8 1.0 %slice_bitcast_fusion = (f32[2,256,256]{2,1,0:T(8,128)}, f32[2,256,256]{2,1,0:T(8,128)}) fusion(f32[2,2,256,256]{3,2,1,0:T(8,128)S(1)} %shard_map.77), kind=kLoop, calls=%fused_computation | loop fusion | bytes 2097152 | tf_op jit(solution)/shard_map/squeeze | solution.py:553

commit v5 on v4

--- a/solution.py
+++ b/solution.py
@@ -469,16 +469,23 @@
         alpha = norm / (product - ratio * norm / alpha_before)
         scal_ref[0] = jnp.broadcast_to(norm, scal_ref.shape[1:])
         scal_ref[1] = jnp.broadcast_to(alpha, scal_ref.shape[1:])
-        row_near.wait_recv()
-        for copy in row_far:
-            pl.when(has_far)(copy.wait_recv)
-        for i in range(n_all):
+        def landed(i):
             pl.when(has_left)(col_right[i].wait_recv)
             pl.when(has_right)(col_left[i].wait_recv)
+
+        row_near.wait_recv()
+        for i in range(n_near):
+            landed(i)
         square = jnp.zeros((1, side), f32)
         going = k + 1 < ITERS
-        for i, (start, size) in enumerate(gather_pieces):
+        for i in (*range(n_far, n_all), *range(n_far)):
+            start, size = gather_pieces[i]
             rows = pl.ds(start, size)
+            if i == 0:
+                for copy in row_far:
+                    pl.when(has_far)(copy.wait_recv)
+            if i < n_far:
+                landed(n_near + i)
             before = field[:, rows, :]
             image = acc_o[:, rows, :] + back_r[:, rows, :] + back_c[:, rows, :]
             direction = before + ratio[None] * d_ref[:, rows, :]
@@ -488,9 +495,10 @@
             left_over = before - alpha[None] * along
             field[:, rows, :] = left_over
             square = square + jnp.sum(left_over * left_over, axis=(0, 1))[None]
-            if i > 0:
+            if 0 < i < n_far:
                 send_piece(i - 1, going)
-        send_piece(n_all - 1, going)
+        for i in range(n_far - 1, n_all):
+            send_piece(i, going)
         scal_ref[2, 0:1, :] = lanes(square)
         for copy in back_near:
             copy.wait_send()

time: 82 us -> 80.5 us (0.982)
  Pallas kernels: 79.5 us -> 78.1 us
    pallas_call x1, Pallas kernels: 79.5 us -> 78.1 us  [local(): pl.pallas_call(functools.partial(kernel, n_row, n_col, cap), out_shape=pl...]
where the time goes in v5:
time: 80.5 us; the launch traced here: 80.4 us
  Pallas kernels  78.1 us (97%)
  between operations  1.29 us (2%)
  local copies, waits for them, and re-layouts  1.03 us (1%)
    pallas_call x1, Pallas kernels, local(): pl.pallas_call(functools.partial(kernel, n_row, n_col, cap), out_shape=pl...  78.1 us

profile of v5, /device:TPU:1, one launch (start us, length us, event | category | flops | bytes accessed | tf_op | source)
XLA Modules:
  0.0 80.4 jit_solution(9908032633933900789)
XLA Ops:
  1.3 78.1 %shard_map.77 = f32[2,2,256,256]{3,2,1,0:T(8,128)S(1)} custom-call(f32[2,256,256]{2,1,0:T(8,128)} %right_hbm.1, f32[2,256,256]{2,1,0:T(8,128)} %probe_hbm.1, f32[256,256]{1,0:T(8,128)} %weights_hbm.1, bf16[8,2,256,128]{3,2,1,0:T(8,128)(2,1)} %constant.2.clone.mats_hbm, s32[2,4]{1,0:T(2,128)} %bitcast.7, s32[1,1]{1,0:T(1,128)S(6)} %copy.8.count_hbm), custom_call_target="tpu_custom_call" | custom-call | tf_op jit(solution)/shard_map/pallas_call | solution.py:529
  79.4 1.0 %slice_bitcast_fusion = (f32[2,256,256]{2,1,0:T(8,128)}, f32[2,256,256]{2,1,0:T(8,128)}) fusion(f32[2,2,256,256]{3,2,1,0:T(8,128)S(1)} %shard_map.77), kind=kLoop, calls=%fused_computation | loop fusion | bytes 2097152 | tf_op jit(solution)/shard_map/squeeze | solution.py:561
